TPU v7x, 32 devices: a whole 2x2x4 slice. The times are simulated.
32 devices in a mesh: tp: 4 (over z), dp: 8 (over y, x, core).
Axes of the slice: x: 2, y: 2, z: 4, core: 2. Of those that a mesh axis runs over, the one named last changes fastest.
Arguments:
- g_qkv: bfloat16 [8, 1024, 32, 3, 80], P('dp', None, 'tp')
- g_out: bfloat16 [8, 2560, 1024], P('dp', 'tp')
- g_up: bfloat16 [8, 1024, 4096], P('dp', None, 'tp')
- g_down: bfloat16 [8, 4096, 1024], P('dp', 'tp')
- g_norms: bfloat16 [8, 6, 1024], P('dp')
- master: float32 [4, 4724736], P('tp', 'dp')
- mom_one: float32 [4, 4724736], P('tp', 'dp')
- mom_two: float32 [4, 4724736], P('tp', 'dp')
Outputs:
- output 1: bfloat16 [1024, 32, 3, 80], P(None, 'tp')
- output 2: bfloat16 [2560, 1024], P('tp')
- output 3: bfloat16 [1024, 4096], P(None, 'tp')
- output 4: bfloat16 [4096, 1024], P('tp')
- output 5: bfloat16 [6, 1024], replicated
- output 6: float32 [4, 4724736], P('tp', 'dp')
- output 7: float32 [4, 4724736], P('tp', 'dp')
- output 8: float32 [4, 4724736], P('tp', 'dp')
- output 9: float32 [], replicated
All inputs are finite; a program needn't handle non-finite values.
Results may differ from a plain program's by a relative error of at most 0.001.
Values are sent between devices in bfloat16 or wider.
A program may use at most 1 GiB of HBM per device.

v0:
```python
import math
import jax
import jax.numpy as jnp
from jax import lax
from jax.sharding import PartitionSpec as P

STEP = 20
BETA_ONE = 0.9
BETA_TWO = 0.95
ADAM_EPS = 1e-8
DECAY = 0.1
LEARN_RATE = 1e-4
MAX_NORM = 1.0
NORM_EPS = 1e-6
BIAS_ONE = 1.0 - BETA_ONE ** STEP
BIAS_TWO = 1.0 - BETA_TWO ** STEP
ARG_SPECS = (P("dp", None, "tp", None, None), P("dp", "tp", None), P("dp", None, "tp"), P("dp", "tp", None), P("dp", None, None), P("tp", "dp"), P("tp", "dp"), P("tp", "dp"))
OUT_SPECS = (P(None, "tp", None, None), P("tp", None), P(None, "tp"), P("tp", None), P(None, None), P("tp", "dp"), P("tp", "dp"), P("tp", "dp"), P())


def adamw_update(grad_clip, master, mom_one, mom_two, is_matrix):
    m_new = BETA_ONE * mom_one + (1.0 - BETA_ONE) * grad_clip
    v_new = BETA_TWO * mom_two + (1.0 - BETA_TWO) * grad_clip * grad_clip
    step_dir = (m_new / BIAS_ONE) / (jnp.sqrt(v_new / BIAS_TWO) + ADAM_EPS)
    master_new = master - LEARN_RATE * (step_dir + jnp.where(is_matrix, DECAY * master, 0.0))
    return master_new, m_new, v_new


def split_params(param_flat, shapes):
    pieces = []
    offset = 0
    for shape in shapes:
        elem_count = math.prod(shape)
        pieces.append(param_flat[offset:offset + elem_count].reshape(shape))
        offset += elem_count
    return tuple(pieces)


def solution(mesh):
    dp_size = mesh.shape["dp"]

    def local_step(g_qkv, g_out, g_up, g_down, g_norms, master, mom_one, mom_two):
        grads = (g_qkv, g_out, g_up, g_down, g_norms)
        shapes = [grad.shape[1:] for grad in grads]
        flat_grad = jnp.concatenate([grad.reshape(-1) for grad in grads])
        flat_count = flat_grad.shape[0]
        mat_count = flat_count - g_norms.size
        part_len = flat_count // dp_size
        received = lax.all_to_all(flat_grad.reshape(dp_size, part_len), "dp", 0, 0, tiled=True)
        grad_mean = jnp.sum(received, axis=0, dtype=jnp.float32) / dp_size
        flat_index = lax.axis_index("dp") * part_len + jnp.arange(part_len)
        is_matrix = flat_index < mat_count
        counted = jnp.logical_or(is_matrix, lax.axis_index("tp") == 0)
        local_sq = jnp.sum(jnp.where(counted, grad_mean * grad_mean, 0.0))
        grad_norm = jnp.sqrt(lax.psum(local_sq, ("tp", "dp")))
        clip = jnp.minimum(1.0, MAX_NORM / (grad_norm + NORM_EPS))
        master_new, m_new, v_new = adamw_update(grad_mean * clip, master[0], mom_one[0], mom_two[0], is_matrix)
        param_flat = lax.all_gather(master_new.astype(jnp.bfloat16), "dp", axis=0, tiled=True)
        params = split_params(param_flat, shapes)
        return params + (master_new[None], m_new[None], v_new[None], grad_norm)

    return jax.shard_map(local_step, mesh=mesh, in_specs=ARG_SPECS, out_specs=OUT_SPECS, check_vma=False)
```

profile of v0, /device:TPU:0, one launch (start us, length us, event | category | flops | bytes accessed | tf_op | source)
XLA Modules:
  0.0 997.1 jit_solution(646378840654542760)
XLA Ops:
  7.2 13.8 %copy.19 = bf16[1,1024,8,3,80]{4,3,2,1,0:T(4,128)(2,1)} copy(bf16[1,1024,8,3,80]{1,4,3,2,0:T(8,128)(2,1)} %param.8) | data formatting | bytes 7864320 | tf_op args[0]
  20.9 18.1 %reshape.114 = bf16[1966080]{0:T(1024)(128)(2,1)} reshape(bf16[1,1024,8,3,80]{4,3,2,1,0:T(4,128)(2,1)} %copy.19) | data formatting | bytes 7864320 | tf_op jit(solution)/shard_map/reshape | solution.py:45
  39.1 3.7 constant_dynamic-update-slice_fusion.4
  43.2 1.2 copy-done.3
  44.4 1.9 copy.23
  47.1 1.2 constant_dynamic-update-slice_fusion.3
  49.1 1.5 constant_dynamic-update-slice_fusion.2
  50.7 1.5 constant_dynamic-update-slice_fusion.1
  52.7 15.2 %all_to_all.8 = bf16[8,1,590592]{2,1,0:T(2,128)(2,1)} reshape(bf16[4724736]{0:T(1024)(128)(2,1)} %constant_dynamic-update-slice_fusion) | data formatting | bytes 18898944 | tf_op jit(solution)/shard_map/all_to_all | solution.py:49
  68.4 202.4 %reduce.7 = bf16[8,590592]{1,0:T(8,128)(2,1)} reduce(bf16[8,1,590592]{2,1,0:T(2,128)(2,1)} %all_to_all.8, bf16[]{:T(256)} %broadcast.77), dimensions={1}, to_apply=%all_to_all.8.reduce_sub_computation | reduce | bytes 18898946 | tf_op jit(solution)/shard_map/all_to_all | solution.py:49
  270.8 19.4 %reshape.126 = bf16[8,2,295296]{2,1,0:T(2,128)(2,1)} reshape(bf16[8,590592]{1,0:T(8,128)(2,1)} %reduce.7) | data formatting | bytes 18898944
  290.2 5.4 all-to-all-start
  295.6 28.0 %multiply_reduce_fusion = (f32[590592]{0:T(1024)}, f32[590592]{0:T(1024)}) fusion(f32[1,590592]{1,0:T(1,128)S(1)} %copy-done.1, f32[1,590592]{1,0:T(1,128)} %param.14), kind=kLoop, calls=%fused_computation.18 | loop fusion | flops 1181184 | bytes 9449472 | tf_op jit(solution)/shard_map/mul | solution.py:23
  323.6 77.8 %all-to-all-done = bf16[8,2,295296]{2,1,0:T(2,128)(2,1)} async-done(((bf16[8,2,295296]{2,1,0:T(2,128)(2,1)}), bf16[8,2,295296]{2,1,0:T(2,128)(2,1)}, u32[]{:S(2)}, u32[]{:S(2)}) %all-to-all-start) | async-done | bytes 9449504 | tf_op jit(solution)/shard_map/all_to_all | solution.py:49
  401.5 30.9 %reshape.127 = bf16[8,1,590592]{2,1,0:T(2,128)(2,1)} reshape(bf16[8,2,295296]{2,1,0:T(2,128)(2,1)} %all-to-all-done) | data formatting | bytes 18898944
  432.3 99.1 %convert_reduce_fusion = f32[590592]{0:T(1024)S(1)} fusion(bf16[8,1,590592]{2,1,0:T(2,128)(2,1)} %reshape.127), kind=kLoop, calls=%fused_computation | loop fusion | flops 8858880 | bytes 11811840 | tf_op jit(solution)/shard_map/reduce_sum | solution.py:50
  531.4 1.4 select_reduce_fusion
  532.8 24.5 %reduce.1 = f32[590592]{0:T(1024)} reduce(f32[1,590592]{1,0:T(1,128)} %param.13, f32[]{:T(128)} %constant.49), dimensions={0}, to_apply=%param.13.reduce_sub_computation | reduce | bytes 4724740 | tf_op args[5]
  557.2 40.4 %psum.7 = f32[]{:T(128)} all-reduce(f32[]{:T(128)} %select_reduce_fusion), channel_id=1, replica_groups=mesh['tp'=4,'dp'=8] {'tp','dp'}, use_global_device_ids=true, to_apply=%region_2.3 | all-reduce | flops 1 | bytes 8 | tf_op jit(solution)/shard_map/psum | solution.py:55
  598.4 6.5 subtract_convert_fusion
  604.9 14.2 %reshape.120 = bf16[1,1,590592]{2,1,0:T(2,128)(2,1)} reshape(bf16[590592]{0:T(1024)(128)(2,1)S(1)} %get-tuple-element.30) | data formatting | bytes 2362368
  619.1 20.8 %multiply_subtract_fusion = (f32[1,590592]{1,0:T(1,128)}, f32[1,590592]{1,0:T(1,128)}, f32[1,590592]{1,0:T(1,128)}) fusion(f32[1,590592]{1,0:T(1,128)} %param.13, s32[]{:T(128)S(6)} %mul.115, f32[590592]{0:T(1024)S(1)} %copy-done, f32[1,590592]{1,0:T(1,128)} %param.14, f32[1,590592]{1,0:T(1,128)} %param.15), kind=kLoop, calls=%fused_computation.16 | loop fusion | flops 10630656 | bytes 16536580 | tf_op jit(solution)/shard_map/sub | solution.py:25
  639.9 78.1 %all-gather.3.cloned.1.call-done = bf16[8,1,590592]{2,1,0:T(2,128)(2,1)} async-done(((bf16[1,1,590592]{2,1,0:T(2,128)(2,1)}), bf16[8,1,590592]{2,1,0:T(2,128)(2,1)}) %all-gather.3.cloned.1.call-update) | async-done | bytes 9449488 | tf_op jit(solution)/shard_map/all_gather | solution.py:58
  718.0 201.5 %reduce.4 = bf16[8,590592]{1,0:T(8,128)(2,1)} reduce(bf16[8,1,590592]{2,1,0:T(2,128)(2,1)} %all-gather.3.cloned.1.call-done, bf16[]{:T(256)} %constant.52), dimensions={1}, to_apply=%all-gather.reduce_sub_computation | reduce | bytes 18898946 | tf_op jit(solution)/shard_map/all_gather | solution.py:58
  919.5 21.6 %reshape.121 = bf16[4724736]{0:T(1024)(128)(2,1)} reshape(bf16[8,590592]{1,0:T(8,128)(2,1)} %reduce.4) | data formatting | bytes 18898944
  941.1 3.8 fusion.10
  944.9 3.6 slice.64
  948.5 4.2 slice.59
  952.7 2.3 slice.61
  954.9 19.4 %reshape.119 = bf16[1024,8,3,80]{3,2,1,0:T(4,128)(2,1)} reshape(bf16[1966080]{0:T(1024)(128)(2,1)} %slice.64) | data formatting | bytes 7864320 | tf_op jit(solution)/shard_map/reshape | solution.py:34
  974.3 12.5 %copy.21 = bf16[1024,8,3,80]{0,3,2,1:T(8,128)(2,1)} copy(bf16[1024,8,3,80]{3,2,1,0:T(4,128)(2,1)} %reshape.119) | data formatting | bytes 7864320
  986.8 1.4 slice.57
  (25 shorter events, 3.8 us)
Async XLA Ops:
  39.0 3.7 copy-start.5
  42.8 1.6 copy-start.3
  43.1 3.2 copy-start.4
  46.3 0.7 copy-start.6
  47.1 2.1 copy-start.2
  290.2 5.4 copy-start.1
  290.2 111.3 %all-to-all-start = ((bf16[8,2,295296]{2,1,0:T(2,128)(2,1)}), bf16[8,2,295296]{2,1,0:T(2,128)(2,1)}, u32[]{:S(2)}, u32[]{:S(2)}) async-start(bf16[8,2,295296]{2,1,0:T(2,128)(2,1)} %reshape.126), calls=%async_computation | async-start | bytes 18898944 | tf_op jit(solution)/shard_map/all_to_all | solution.py:49
  295.6 422.5 %all-gather.3.cloned.1.call-start = ((), (), s32[]{:S(2)}) async-start(), calls=%async_computation.1 | async-start | bytes 21261312 | tf_op jit(solution)/shard_map/all_gather | solution.py:58
  604.9 14.2 %copy-start = (f32[590592]{0:T(1024)S(1)}, f32[590592]{0:T(1024)}, u32[]{:S(2)}) copy-start(f32[590592]{0:T(1024)} %get-tuple-element.31) | copy-start | bytes 7087108
  974.3 12.5 %slice-start = ((bf16[4724736]{0:T(1024)(128)(2,1)}), bf16[655360]{0:T(1024)(128)(2,1)S(1)}, s32[]{:S(2)}) async-start(bf16[4724736]{0:T(1024)(128)(2,1)} %reshape.121), calls=%async_computation.2 | async-start | bytes 2621440 | tf_op jit(solution)/shard_map/slice | solution.py:34
  986.8 1.4 slice-start.1
Sparse Core Ops, SparseCore 0:
  619.2 98.7 all-gather.2
where the time goes:
time: 1010 us; the launch traced here: 997 us
  other arithmetic  584 us (58%)
  local copies, waits for them, and re-layouts  195 us (19%)
  waiting for transfers between devices  156 us (15%)
  blocking collectives  40.4 us (4%)
  between operations  16.2 us (2%)
    all_to_all x1, other arithmetic, local_step(): lax.all_to_all(flat_grad.reshape(dp_size, part_len), 'dp', 0, 0, tiled=True)  202 us
    all_gather x1, other arithmetic, local_step(): lax.all_gather(master_new.astype(jnp.bfloat16), 'dp', axis=0, tiled=True)  202 us
    unnamed x27, local copies, waits for them, and re-layouts  125 us
    reduce_sum x1, other arithmetic, local_step(): grad_mean = jnp.sum(received, axis=0, dtype=jnp.float32) / dp_size  99.1 us
    all_gather x1, waiting for transfers between devices, local_step(): lax.all_gather(master_new.astype(jnp.bfloat16), 'dp', axis=0, tiled=True)  78.1 us
    all_to_all x1, waiting for transfers between devices, local_step(): lax.all_to_all(flat_grad.reshape(dp_size, part_len), 'dp', 0, 0, tiled=True)  77.8 us
    psum x1, blocking collectives, local_step(): grad_norm = jnp.sqrt(lax.psum(local_sq, ('tp', 'dp')))  40.4 us
    mul x1, other arithmetic, adamw_update(): v_new = BETA_TWO * mom_two + (1.0 - BETA_TWO) * grad_clip * grad_clip  28 us
  transfers between devices with their start and end apart: 2, of which 2 were waited for; matrix products, arithmetic and copies ran while one was open for 5% of the time, Pallas kernels for 0%

commit v1 on v0

v1 whole, which is shorter than its diff:
```python
import functools

import jax
import jax.numpy as jnp
from jax import lax
from jax.experimental import pallas as pl
from jax.experimental.pallas import tpu as pltpu
from jax.sharding import PartitionSpec as P

STEP = 20
BETA_ONE = 0.9
BETA_TWO = 0.95
ADAM_EPS = 1e-8
DECAY = 0.1
LEARN_RATE = 1e-4
MAX_NORM = 1.0
NORM_EPS = 1e-6
BIAS_ONE = 1.0 - BETA_ONE ** STEP
BIAS_TWO = 1.0 - BETA_TWO ** STEP
ARG_SPECS = (P("dp", None, "tp", None, None), P("dp", "tp", None), P("dp", None, "tp"), P("dp", "tp", None), P("dp", None, None), P("tp", "dp"), P("tp", "dp"), P("tp", "dp"))
OUT_SPECS = (P(None, "tp", None, None), P("tp", None), P(None, "tp"), P("tp", None), P(None, None), P("tp", "dp"), P("tp", "dp"), P("tp", "dp"), P())

MESH = pl.DeviceIdType.MESH
F32 = jnp.float32
BF16 = jnp.bfloat16

Q_TILES = 1920
TILES = 4616
Q_COLS = 15
M_COLS = 8
PART_ROWS = 4614
MAT_ROWS = 36864
WIN = 600
HALF = WIN // 2
WIN_START = (0, 570, 1140, 1725, 2304, 2880, 3456, 4016)
EMIT_START = (0, 585, 1155, 1740, 2312, 2888, 3464, 4040)
EMIT_END = (585, 1155, 1740, 2312, 2888, 3464, 4040, 4616)
Q_BLOCKS = (40, 40, 40, 13, 0, 0, 0, 0)
M_BLOCKS = (0, 0, 0, 50, 75, 75, 75, 75)
EMIT = 588
STATE_BASE = 176
STATE_ROWS = 4984
HALO = 80

K_RS = 5
N_RS = HALF // K_RS
K_AG = 6
N_AG = EMIT // K_AG
STEP_TILES = 4


def pick(values, y, x, c):
    total = 0
    for index, value in enumerate(values):
        if value:
            term = value
            for shift, bit in ((2, y), (1, x), (0, c)):
                term = term * (bit if (index >> shift) & 1 else 1 - bit)
            total = total + term
    return total


def step_kernel(gq, go, gu, gd, gn, w_in, m_in, v_in,
                ag, w_out, m_out, v_out, norm_out,
                grads, r_ra, r_rb, r_da, r_db, r_pf, r_pa, r_pb,
                r_sa, r_sb, s_sa, s_sb, gsum, mask, state, halo, pbuf, nb1, nb2,
                load_sem, store_sem, own_sem,
                ss_raw, rs_raw, ss_pf, rs_pf, ss_pp, rs_pp, ss_s, rs_s,
                ss_h, rs_h, ss_n1, rs_n1, ss_n2, rs_n2,
                ss_own, rs_own, ss_rel, rs_rel, ss_d2d, rs_d2d):
    dp = lax.axis_index("dp")
    tp = lax.axis_index("tp")
    y = dp // 4
    x = dp // 2 % 2
    c = dp % 2

    def at(yy, xx, cc):
        return {"dp": yy * 4 + xx * 2 + cc}

    def win(yy, xx, cc):
        return pick(WIN_START, yy, xx, cc)

    ny, nx, nc = 1 - y, 1 - x, 1 - c

    def remote(src, dst, ssem, rsem, dev):
        return pltpu.make_async_remote_copy(
            src_ref=src, dst_ref=dst, send_sem=ssem, recv_sem=rsem, device_id=dev, device_id_type=MESH)

    loads = []
    for index, (src, start, count) in enumerate((
            (gq, 0, 1920), (go, 1920, 640), (gu, 2560, 1024), (gd, 3584, 1024), (gn, 4608, 8))):
        loads.append(pltpu.make_async_copy(src, grads.at[pl.ds(start, count)], load_sem.at[index]))
    state_loads = []
    for index, src in enumerate((w_in, m_in, v_in)):
        state_loads.append(pltpu.make_async_copy(
            src, state.at[index, pl.ds(STATE_BASE, PART_ROWS)], load_sem.at[5 + index]))
    for copy in loads:
        copy.start()
    barrier = pltpu.get_barrier_semaphore()
    for offset in range(1, 8):
        pl.semaphore_signal(barrier, inc=1, device_id={"dp": (dp + offset) % 8}, device_id_type=MESH)
    for offset in range(1, 4):
        pl.semaphore_signal(barrier, inc=1, device_id={"tp": (tp + offset) % 4}, device_id_type=MESH)
    pl.semaphore_wait(barrier, 10)
    for copy in loads:
        copy.wait()

    def cut(start, k, n=N_RS):
        return pl.ds(start + k * n, n)

    raw_bufs = (r_ra, r_rb, r_da, r_db)

    def raw(stream, cc, k, slot):
        to_y = stream in (0, 2)
        half = 0 if to_y else HALF
        if stream < 2:
            start = win(ny, nx, cc)
        elif to_y:
            start = win(ny, x, cc)
        else:
            start = win(y, nx, cc)
        dev = at(ny, x, cc) if to_y else at(y, nx, cc)
        return remote(grads.at[cut(start + half, k)], raw_bufs[stream].at[slot, cut(0, k)],
                      ss_raw.at[stream, cc, k], rs_raw.at[stream, slot, k], dev)

    def partner_final(k):
        return remote(grads.at[cut(win(y, x, nc), k)], r_pf.at[cut(0, k)], ss_pf.at[k], rs_pf.at[k], at(y, x, nc))

    def partner_relay(which, k):
        if which == 0:
            start, dst = win(y, nx, nc), r_pa
        else:
            start, dst = win(ny, x, nc) + HALF, r_pb
        return remote(grads.at[cut(start, k)], dst.at[cut(0, k)], ss_pp.at[which, k], rs_pp.at[which, k], at(y, x, nc))

    def relayed(which, k):
        src, dst, dev = (s_sa, r_sa, at(y, nx, c)) if which == 0 else (s_sb, r_sb, at(ny, x, c))
        return remote(src.at[cut(0, k)], dst.at[cut(0, k)], ss_s.at[which, k], rs_s.at[which, k], dev)

    def halo_copy(index):
        src = (w_in, m_in, v_in)[index]
        return remote(src.at[pl.ds(0, HALO)], halo.at[index],
                      ss_h.at[index], rs_h.at[index], {"dp": (dp + 7) % 8})

    def send_relay_raw(k, carry):
        for cc in range(2):
            raw(0, cc, k, c).start()
            raw(1, cc, k, c).start()
        partner_relay(0, k).start()
        partner_relay(1, k).start()
        return carry

    def send_direct_raw(k, carry):
        for cc in range(2):
            raw(2, cc, k, c).start()
            raw(3, cc, k, c).start()
        partner_final(k).start()
        partner_final(k + K_RS).start()
        return carry

    lax.fori_loop(0, K_RS, send_relay_raw, 0)
    lax.fori_loop(0, K_RS, send_direct_raw, 0)
    for index in range(3):
        halo_copy(index).start()
    for copy in state_loads:
        copy.start()

    off = PART_ROWS * dp - 8 * win(y, x, c)
    mat_end = MAT_ROWS - 8 * win(y, x, c)
    last = jnp.minimum(off + PART_ROWS, mat_end + jnp.where(tp == 0, 48, 0))
    q_blocks = pick(Q_BLOCKS, y, x, c)
    m_blocks = pick(M_BLOCKS, y, x, c)
    row = lax.broadcasted_iota(jnp.int32, (8, 128), 0)
    for index in range(WIN - 5, WIN):
        mask[index] = jnp.zeros((8, 128), F32)

    def mask_blocks(columns, tile0):
        def body(block, carry):
            for col in range(columns):
                tile = tile0 + block * columns + col
                lane_row = row * columns + (tile0 * 8 + block * columns * 8 + col)
                inside = jnp.logical_and(lane_row >= off, lane_row < last)
                mask[tile] = jnp.where(inside, 1.0, 0.0)
            return carry
        return body

    lax.fori_loop(0, q_blocks, mask_blocks(Q_COLS, 0), 0)
    lax.fori_loop(0, m_blocks, mask_blocks(M_COLS, q_blocks * Q_COLS), 0)

    def relay(which):
        own_start = win(y, nx, c) if which == 0 else win(ny, x, c) + HALF
        raw_buf, pair_buf, out_buf = (r_ra, r_pa, s_sa) if which == 0 else (r_rb, r_pb, s_sb)

        def body(k):
            raw(which, 0, k, 0).wait_recv()
            raw(which, 1, k, 1).wait_recv()
            partner_relay(which, k).wait_recv()

            def tiles(index, carry):
                here = pl.ds(k * N_RS + index * STEP_TILES, STEP_TILES)
                total = grads[pl.ds(own_start + k * N_RS + index * STEP_TILES, STEP_TILES)].astype(F32)
                total = total + pair_buf[here].astype(F32)
                total = total + raw_buf[0, here].astype(F32)
                total = total + raw_buf[1, here].astype(F32)
                out_buf[here] = total
                return carry

            lax.fori_loop(0, N_RS // STEP_TILES, tiles, 0)
            relayed(which, k).start()
        return body

    relay_a, relay_b = relay(0), relay(1)

    def relay_step(k, carry):
        relay_a(k)
        relay_b(k)
        return carry

    lax.fori_loop(0, K_RS, relay_step, 0)

    for copy in state_loads:
        copy.wait()
    for index in range(3):
        halo_copy(index).wait_recv()
        state[index, pl.ds(STATE_BASE + PART_ROWS, HALO)] = halo[index]

    def finish(which):
        half = 0 if which == 0 else HALF
        raw_buf, sum_buf = (r_da, r_sa) if which == 0 else (r_db, r_sb)

        def body(k, acc):
            raw(2 + which, 0, k, 0).wait_recv()
            raw(2 + which, 1, k, 1).wait_recv()
            partner_final(k + which * K_RS).wait_recv()
            relayed(which, k).wait_recv()

            def tiles(index, acc):
                here = pl.ds(k * N_RS + index * STEP_TILES, STEP_TILES)
                part = pl.ds(half + k * N_RS + index * STEP_TILES, STEP_TILES)
                total = grads[pl.ds(win(y, x, c) + half + k * N_RS + index * STEP_TILES, STEP_TILES)].astype(F32)
                total = total + r_pf[part].astype(F32)
                total = total + raw_buf[0, here].astype(F32)
                total = total + raw_buf[1, here].astype(F32)
                total = (total + sum_buf[here]) * 0.125
                gsum[part] = total
                square = jnp.where(mask[part] > 0.5, total * total, 0.0)
                return acc + jnp.sum(square, axis=0)

            return lax.fori_loop(0, N_RS // STEP_TILES, tiles, acc)
        return body

    finish_a, finish_b = finish(0), finish(1)
    acc = lax.fori_loop(0, K_RS, lambda k, acc: finish_b(k, finish_a(k, acc)), jnp.zeros((8, 128), F32))

    nb1[dp] = acc

    def norm_plane(offset):
        return remote(nb1.at[dp], nb1.at[dp], ss_n1.at[offset], rs_n1.at[dp], {"dp": (dp + offset) % 8})

    def norm_plane_in(offset):
        source = (dp + offset) % 8
        return remote(nb1.at[dp], nb1.at[source], ss_n1.at[offset], rs_n1.at[source], {"dp": source})

    def norm_line(offset):
        return remote(nb2.at[tp], nb2.at[tp], ss_n2.at[offset], rs_n2.at[tp], {"tp": (tp + offset) % 4})

    def norm_line_in(offset):
        source = (tp + offset) % 4
        return remote(nb2.at[tp], nb2.at[source], ss_n2.at[offset], rs_n2.at[source], {"tp": source})

    for offset in range(1, 8):
        norm_plane(offset).start()
    for offset in range(1, 8):
        norm_plane_in(offset).wait_recv()
    plane = nb1[0]
    for index in range(1, 8):
        plane = plane + nb1[index]
    nb2[tp] = plane
    for offset in range(1, 4):
        norm_line(offset).start()
    for offset in range(1, 4):
        norm_line_in(offset).wait_recv()
    total = nb2[0] + nb2[1] + nb2[2] + nb2[3]
    total = jnp.sum(jnp.sum(total, axis=0, keepdims=True), axis=1, keepdims=True)
    norm = jnp.sqrt(jnp.broadcast_to(total, (8, 128)))
    norm_out[...] = norm
    clip = jnp.minimum(1.0, MAX_NORM / (norm + NORM_EPS))

    def update_blocks(columns, tile0):
        def body(block, carry):
            row0 = tile0 * 8 + block * columns * 8
            decay = jnp.where(row0 < mat_end, DECAY, 0.0)
            for col in range(columns):
                tile = tile0 + block * columns + col
                here = pl.ds(STATE_BASE - off + row0 + col, 8, stride=columns)
                grad = gsum[tile] * clip
                w_old = state[0, here]
                m_new = BETA_ONE * state[1, here] + (1.0 - BETA_ONE) * grad
                v_new = BETA_TWO * state[2, here] + (1.0 - BETA_TWO) * grad * grad
                step_dir = (m_new * (1.0 / BIAS_ONE)) / (jnp.sqrt(v_new * (1.0 / BIAS_TWO)) + ADAM_EPS)
                w_new = w_old - LEARN_RATE * (step_dir + decay * w_old)
                state[0, here] = w_new
                state[1, here] = m_new
                state[2, here] = v_new
                pbuf[tile] = w_new.astype(BF16)
            return carry
        return body

    lax.fori_loop(0, q_blocks, update_blocks(Q_COLS, 0), 0)
    lax.fori_loop(0, m_blocks, update_blocks(M_COLS, q_blocks * Q_COLS), 0)

    emit0 = pick([e - s for e, s in zip(EMIT_START, WIN_START)], y, x, c)

    def piece(k):
        return pl.ds(k * N_AG, N_AG)

    def own_out(which, k):
        dev = (at(y, nx, c), at(ny, x, c), at(y, x, nc))[which]
        return remote(pbuf.at[pl.ds(emit0 + k * N_AG, N_AG)], ag.at[dp, piece(k)],
                      ss_own.at[which, k], rs_own.at[which, k], dev)

    def own_in(which, k):
        part = (y * 4 + nx * 2 + c, ny * 4 + x * 2 + c, y * 4 + x * 2 + nc)[which]
        dev = (at(y, nx, c), at(ny, x, c), at(y, x, nc))[which]
        return remote(ag.at[part, piece(k)], ag.at[part, piece(k)], ss_own.at[which, k], rs_own.at[which, k], dev)

    def pass_out(which, k):
        if which == 0:
            part, dev = y * 4 + nx * 2 + c, at(ny, x, c)
        else:
            part, dev = ny * 4 + x * 2 + c, at(y, nx, c)
        return remote(ag.at[part, piece(k)], ag.at[part, piece(k)], ss_rel.at[k], rs_rel.at[k], dev)

    def pass_in(which, k):
        part = ny * 4 + nx * 2 + c
        dev = at(ny, x, c) if which == 0 else at(y, nx, c)
        return remote(ag.at[part, piece(k)], ag.at[part, piece(k)], ss_rel.at[k], rs_rel.at[k], dev)

    def pair_out(which, k):
        part = (y * 4 + nx * 2 + c, ny * 4 + x * 2 + c, ny * 4 + nx * 2 + c)[which]
        return remote(ag.at[part, piece(k)], ag.at[part, piece(k)], ss_d2d.at[which, k], rs_d2d.at[which, k], at(y, x, nc))

    def pair_in(which, k):
        part = (y * 4 + nx * 2 + nc, ny * 4 + x * 2 + nc, ny * 4 + nx * 2 + nc)[which]
        return remote(ag.at[part, piece(k)], ag.at[part, piece(k)], ss_d2d.at[which, k], rs_d2d.at[which, k], at(y, x, nc))

    own_copy = pltpu.make_async_copy(pbuf.at[pl.ds(emit0, EMIT)], ag.at[dp], own_sem)
    half_ag = K_AG // 2

    def send_own(index, carry):
        own_out(0, index).start()
        own_out(1, (index + half_ag) % K_AG).start()
        return carry

    lax.fori_loop(0, K_AG, send_own, 0)
    own_copy.start()
    lax.fori_loop(0, K_AG, lambda k, carry: (own_out(2, k).start(), carry)[1], 0)
    stores = []
    for index, dst in enumerate((w_out, m_out, v_out)):
        stores.append(pltpu.make_async_copy(
            state.at[index, pl.ds(STATE_BASE, PART_ROWS)], dst, store_sem.at[index]))
        stores[-1].start()

    def first_half(k, carry):
        own_in(0, k).wait_recv()
        pass_out(0, k).start()
        pair_out(0, k).start()
        own_in(1, k + half_ag).wait_recv()
        pass_out(1, k + half_ag).start()
        pair_out(1, k + half_ag).start()
        return carry

    def second_half(k, carry):
        own_in(0, k + half_ag).wait_recv()
        pair_out(0, k + half_ag).start()
        own_in(1, k).wait_recv()
        pair_out(1, k).start()
        return carry

    def diagonal(k, carry):
        pass_in(0, k).wait_recv()
        pair_out(2, k).start()
        pass_in(1, k + half_ag).wait_recv()
        pair_out(2, k + half_ag).start()
        return carry

    lax.fori_loop(0, half_ag, first_half, 0)
    lax.fori_loop(0, half_ag, second_half, 0)
    lax.fori_loop(0, half_ag, diagonal, 0)

    def drain_ag(k, carry):
        own_in(2, k).wait_recv()
        for which in range(3):
            pair_in(which, k).wait_recv()
            pair_out(which, k).wait_send()
            own_out(which, k).wait_send()
        return carry

    lax.fori_loop(0, K_AG, drain_ag, 0)

    def drain_half(k, carry):
        pass_out(0, k).wait_send()
        pass_out(1, k + half_ag).wait_send()
        return carry

    lax.fori_loop(0, half_ag, drain_half, 0)

    def drain_rs(k, carry):
        for stream in range(4):
            for cc in range(2):
                raw(stream, cc, k, c).wait_send()
        partner_final(k).wait_send()
        partner_final(k + K_RS).wait_send()
        for which in range(2):
            partner_relay(which, k).wait_send()
            relayed(which, k).wait_send()
        return carry

    lax.fori_loop(0, K_RS, drain_rs, 0)
    for index in range(3):
        halo_copy(index).wait_send()
    for offset in range(1, 8):
        norm_plane(offset).wait_send()
    for offset in range(1, 4):
        norm_line(offset).wait_send()
    own_copy.wait()
    for copy in stores:
        copy.wait()


def lay_out_kernel(ag, q_out, o_out, u_out, d_out, n_out, tiles, in_sem, out_sem):
    loads = []
    for part in range(8):
        start, end = EMIT_START[part], EMIT_END[part]
        loads.append(pltpu.make_async_copy(
            ag.at[part, pl.ds(0, end - start)], tiles.at[pl.ds(start, end - start)], in_sem.at[part]))
        loads[-1].start()
    outs = []
    for index, (dst, start, count) in enumerate((
            (q_out, 0, 1920), (o_out, 1920, 640), (u_out, 2560, 1024), (d_out, 3584, 1024), (n_out, 4608, 8))):
        outs.append(pltpu.make_async_copy(tiles.at[pl.ds(start, count)], dst, out_sem.at[index]))
    for part in range(8):
        loads[part].wait()
        if part == 3:
            outs[0].start()
        if part == 5:
            outs[1].start()
        if part == 6:
            outs[2].start()
    outs[3].start()
    outs[4].start()
    for copy in outs:
        copy.wait()


def to_tiles(matrix):
    rows, cols = matrix.shape
    return matrix.reshape(rows // 8, 8, cols // 128, 128).transpose(0, 2, 1, 3).reshape(rows * cols // 1024, 8, 128)


def from_tiles(tiles, rows, cols):
    return tiles.reshape(rows // 8, cols // 128, 8, 128).transpose(0, 2, 1, 3).reshape(rows, cols)


def any_spec(count):
    return [pl.BlockSpec(memory_space=pl.ANY)] * count


def solution(mesh):
    dma = pltpu.SemaphoreType.DMA

    def local_step(g_qkv, g_out, g_up, g_down, g_norms, master, mom_one, mom_two):
        gq = to_tiles(g_qkv[0].transpose(1, 2, 3, 0).reshape(1920, 1024).T)
        go, gu, gd = to_tiles(g_out[0]), to_tiles(g_up[0]), to_tiles(g_down[0])
        gn = to_tiles(jnp.pad(g_norms[0], ((0, 2), (0, 0))))
        part = jax.ShapeDtypeStruct((PART_ROWS, 128), F32)
        scratch = [
            pltpu.VMEM((TILES, 8, 128), BF16),
            *[pltpu.VMEM((2, HALF, 8, 128), BF16)] * 4,
            pltpu.VMEM((WIN, 8, 128), BF16),
            *[pltpu.VMEM((HALF, 8, 128), BF16)] * 2,
            *[pltpu.VMEM((HALF, 8, 128), F32)] * 4,
            pltpu.VMEM((WIN, 8, 128), F32),
            pltpu.VMEM((WIN, 8, 128), F32),
            pltpu.VMEM((3, STATE_ROWS, 128), F32),
            pltpu.VMEM((3, HALO, 128), F32),
            pltpu.VMEM((616, 8, 128), BF16),
            pltpu.VMEM((8, 8, 128), F32),
            pltpu.VMEM((4, 8, 128), F32),
            dma((8,)), dma((3,)), dma(()),
            dma((4, 2, K_RS)), dma((4, 2, K_RS)),
            dma((2 * K_RS,)), dma((2 * K_RS,)),
            dma((2, K_RS)), dma((2, K_RS)),
            dma((2, K_RS)), dma((2, K_RS)),
            dma((3,)), dma((3,)),
            dma((8,)), dma((8,)),
            dma((4,)), dma((4,)),
            dma((3, K_AG)), dma((3, K_AG)),
            dma((K_AG,)), dma((K_AG,)),
            dma((3, K_AG)), dma((3, K_AG)),
        ]
        ag, w_new, m_new, v_new, norm = pl.pallas_call(
            step_kernel,
            name="reduce_update_gather",
            out_shape=[jax.ShapeDtypeStruct((8, EMIT, 8, 128), BF16), part, part, part,
                       jax.ShapeDtypeStruct((8, 128), F32)],
            in_specs=any_spec(8),
            out_specs=any_spec(4) + [pl.BlockSpec(memory_space=pltpu.VMEM)],
            scratch_shapes=scratch,
            compiler_params=pltpu.CompilerParams(
                collective_id=0, has_side_effects=True, vmem_limit_bytes=60 * 1024 * 1024),
        )(gq, go, gu, gd, gn, *[a.reshape(PART_ROWS, 128) for a in (master, mom_one, mom_two)])
        w_new, m_new, v_new = [a.reshape(master.shape) for a in (w_new, m_new, v_new)]
        pq, po, pu, pd, pn = pl.pallas_call(
            lay_out_kernel,
            name="lay_out",
            out_shape=[jax.ShapeDtypeStruct((count, 8, 128), BF16) for count in (1920, 640, 1024, 1024, 8)],
            in_specs=any_spec(1),
            out_specs=any_spec(5),
            scratch_shapes=[pltpu.VMEM((TILES, 8, 128), BF16), dma((8,)), dma((5,))],
            compiler_params=pltpu.CompilerParams(vmem_limit_bytes=32 * 1024 * 1024),
        )(ag)
        p_qkv = from_tiles(pq, 1024, 1920).T.reshape(8, 3, 80, 1024).transpose(3, 0, 1, 2)
        return (p_qkv, from_tiles(po, 640, 1024), from_tiles(pu, 1024, 1024), from_tiles(pd, 1024, 1024),
                from_tiles(pn, 8, 1024)[:6], w_new, m_new, v_new, norm[0, 0])

    return jax.shard_map(local_step, mesh=mesh, in_specs=ARG_SPECS, out_specs=OUT_SPECS, check_vma=False)
```

time: 1010 us -> 279 us (0.28); the launches traced: 997 us -> 279 us
  other arithmetic: 584 us -> 72.7 us
  waiting for transfers between devices: 156 us -> 0 us
  Pallas kernels: 0 us -> 151 us
  local copies, waits for them, and re-layouts: 195 us -> 54.9 us
  blocking collectives: 40.4 us -> 0 us
  between operations: 16.2 us -> 0.68 us
    all_to_all x1 -> x0, other arithmetic: 202 us -> none  [local_step(): lax.all_to_all(flat_grad.reshape(dp_size, part_len), 'dp', 0, 0, tiled=True)]
    all_gather x1 -> x0, other arithmetic: 202 us -> none  [local_step(): lax.all_gather(master_new.astype(jnp.bfloat16), 'dp', axis=0, tiled=True)]
    pallas_call x0 -> x2, Pallas kernels: none -> 151 us  [the longest x1 146 us: local_step(): pl.pallas_call(step_kernel, name='reduce_update_gather', out_shape=[jax.S...]
    unnamed x27 -> x13, local copies, waits for them, and re-layouts: 125 us -> 21.1 us
    reduce_sum x2 -> x0, other arithmetic: 100 us -> none  [the longest x1 99.1 us: local_step(): grad_mean = jnp.sum(received, axis=0, dtype=jnp.float32) / dp_size]
    all_gather x1 -> x0, waiting for transfers between devices: 78.1 us -> none  [local_step(): lax.all_gather(master_new.astype(jnp.bfloat16), 'dp', axis=0, tiled=True)]
    all_to_all x1 -> x0, waiting for transfers between devices: 77.8 us -> none  [local_step(): lax.all_to_all(flat_grad.reshape(dp_size, part_len), 'dp', 0, 0, tiled=True)]
    unnamed x1 -> x3, other arithmetic: 24.5 us -> 72.7 us
  transfers between devices with their start and end apart: 2 -> 0, of which waited for: 2 -> 0; matrix products, arithmetic and copies ran while one was open for 5% -> 0% of each run, Pallas kernels for 0% -> 0%
where the time goes in v1:
time: 279 us
  Pallas kernels  151 us (54%)
  other arithmetic  72.7 us (26%)
  local copies, waits for them, and re-layouts  54.9 us (20%)
    pallas_call x1, Pallas kernels, local_step(): pl.pallas_call(step_kernel, name='reduce_update_gather', out_shape=[jax.S...  146 us
    unnamed x3, other arithmetic  72.7 us
    unnamed x13, local copies, waits for them, and re-layouts  21.1 us
    reshape x1, local copies, waits for them, and re-layouts, local_step(): a.reshape(master.shape)  18 us
    transpose x1, local copies, waits for them, and re-layouts, local_step(): from_tiles(pq, 1024, 1920).T.reshape(8, 3, 80, 1024).transpose(3, 0, 1, 2)  6.42 us
    transpose x1, local copies, waits for them, and re-layouts, local_step(): gq = to_tiles(g_qkv[0].transpose(1, 2, 3, 0).reshape(1920, 1024).T)  6.27 us

profile of v1, /device:TPU:0, one launch (start us, length us, event | category | flops | bytes accessed | tf_op | source)
XLA Modules:
  0.0 278.8 jit_solution(3267431217673995239)
XLA Ops:
  0.6 1.3 pad_bitcast_fusion.gn
  2.0 0.0 copy-start.5
  2.0 24.6 %reduce = f32[590592]{0:T(1024)} reduce(f32[1,590592]{1,0:T(1,128)} %param.13, f32[]{:T(128)} %constant.13), dimensions={0}, to_apply=%param.13.reduce_sub_computation | reduce | bytes 4724740 | tf_op args[5]
  26.6 0.0 copy-done.5
  26.6 23.4 %reduce.1 = f32[590592]{0:T(1024)} reduce(f32[1,590592]{1,0:T(1,128)S(1)} %copy-done.5, f32[]{:T(128)} %constant.13), dimensions={0}, to_apply=%param.14.reduce_sub_computation | reduce | bytes 4724740 | tf_op args[6]
  50.0 24.7 %reduce.2 = f32[590592]{0:T(1024)} reduce(f32[1,590592]{1,0:T(1,128)} %param.15, f32[]{:T(128)} %constant.13), dimensions={0}, to_apply=%param.15.reduce_sub_computation | reduce | bytes 4724740 | tf_op args[7]
  74.7 6.3 %copy.19 = bf16[1024,1920]{1,0:T(8,128)(2,1)} copy(bf16[1024,1920]{0,1:T(8,128)(2,1)} %bitcast.87) | data formatting | bytes 7864320 | tf_op jit(solution)/shard_map/transpose | solution.py:473
  80.9 145.8 %reduce_update_gather.1 = (bf16[8,588,8,128]{3,2,1,0:T(8,128)(2,1)}, f32[4614,128]{1,0:T(8,128)}, f32[4614,128]{1,0:T(8,128)}, f32[4614,128]{1,0:T(8,128)}, f32[8,128]{1,0:T(8,128)}) custom-call(bf16[1920,8,128]{2,1,0:T(8,128)(2,1)} %bitcast.83, bf16[640,8,128]{2,1,0:T(8,128)(2,1)} %bitcast.95, bf16[1024,8,128]{2,1,0:T(8,128)(2,1)} %bitcast.93, ...), custom_call_target="tpu_custom_call" | custom-call | tf_op jit(solution)/shard_map/reduce_update_gather/pallas_call | solution.py:502
  226.7 1.2 slice.11
  227.9 0.0 copy-start
  227.9 3.7 %copy-done = bf16[8,588,8,128]{3,2,1,0:T(8,128)(2,1)S(1)} copy-done((bf16[8,588,8,128]{3,2,1,0:T(8,128)(2,1)S(1)}, bf16[8,588,8,128]{3,2,1,0:T(8,128)(2,1)}, u32[]{:S(2)}) %copy-start) | copy-done | bytes 9633816
  231.7 4.8 %lay_out.1 = (bf16[1920,8,128]{2,1,0:T(8,128)(2,1)S(1)}, bf16[640,8,128]{2,1,0:T(8,128)(2,1)}, bf16[1024,8,128]{2,1,0:T(8,128)(2,1)}, bf16[1024,8,128]{2,1,0:T(8,128)(2,1)}, bf16[8,8,128]{2,1,0:T(8,128)(2,1)S(1)}) custom-call(bf16[8,588,8,128]{3,2,1,0:T(8,128)(2,1)S(1)} %copy-done), custom_call_target="tpu_custom_call" | custom-call | tf_op jit(solution)/shard_map/lay_out/pallas_call | solution.py:514
  236.4 0.0 copy-start.1
  236.4 1.9 copy-done.1
  238.3 0.0 copy-start.2
  238.3 6.4 %copy.20 = bf16[1920,1024]{1,0:T(8,128)(2,1)} copy(bf16[1920,1024]{0,1:T(8,128)(2,1)} %bitcast.81) | data formatting | bytes 7864320 | tf_op jit(solution)/shard_map/transpose | solution.py:523
  244.7 0.0 copy-done.2
  244.7 0.0 copy-start.3
  244.7 0.0 copy-start.4
  244.7 15.4 %copy.27 = f32[1,1,4614,128]{3,1,2,0:T(1,128)} copy(f32[1,1,4614,128]{3,2,1,0:T(8,128)S(1)} %bitcast.89) | data formatting | bytes 4724736
  260.2 0.6 slice_bitcast_fusion
  260.8 0.0 copy-done.3
  260.8 0.0 copy-done.4
  260.8 18.0 %copy_bitcast_fusion = (f32[1,590592]{1,0:T(1,128)}, f32[1,590592]{1,0:T(1,128)}) fusion(f32[1,1,4614,128]{3,2,1,0:T(8,128)S(1)} %bitcast.91, f32[1,1,4614,128]{3,2,1,0:T(8,128)S(1)} %bitcast.90), kind=kLoop, calls=%fused_computation | loop fusion | bytes 9449472 | tf_op jit(solution)/shard_map/reshape | solution.py:513
Async XLA Ops:
  2.0 24.6 %copy-start.5 = (f32[1,590592]{1,0:T(1,128)S(1)}, f32[1,590592]{1,0:T(1,128)}, u32[]{:S(2)}) copy-start(f32[1,590592]{1,0:T(1,128)} %param.14) | copy-start | bytes 7087108
  227.9 3.7 %copy-start = (bf16[8,588,8,128]{3,2,1,0:T(8,128)(2,1)S(1)}, bf16[8,588,8,128]{3,2,1,0:T(8,128)(2,1)}, u32[]{:S(2)}) copy-start(bf16[8,588,8,128]{3,2,1,0:T(8,128)(2,1)} %get-tuple-element.19.ag) | copy-start | bytes 28901380
  236.4 1.9 copy-start.1
  238.3 6.4 %copy-start.2 = (f32[4614,128]{1,0:T(8,128)S(1)}, f32[4614,128]{1,0:T(8,128)}, u32[]{:S(2)}) copy-start(f32[4614,128]{1,0:T(8,128)} %get-tuple-element.25) | copy-start | bytes 7087108
  244.7 16.1 %copy-start.3 = (f32[4614,128]{1,0:T(8,128)S(1)}, f32[4614,128]{1,0:T(8,128)}, u32[]{:S(2)}) copy-start(f32[4614,128]{1,0:T(8,128)} %get-tuple-element.26) | copy-start | bytes 7087108
  244.7 16.1 %copy-start.4 = (f32[4614,128]{1,0:T(8,128)S(1)}, f32[4614,128]{1,0:T(8,128)}, u32[]{:S(2)}) copy-start(f32[4614,128]{1,0:T(8,128)} %get-tuple-element.27) | copy-start | bytes 7087108

commit v2 on v0

v2 whole, which is shorter than its diff:
```python
import functools

import jax
import jax.numpy as jnp
from jax import lax
from jax.experimental import pallas as pl
from jax.experimental.pallas import tpu as pltpu
from jax.sharding import PartitionSpec as P

STEP = 20
BETA_ONE = 0.9
BETA_TWO = 0.95
ADAM_EPS = 1e-8
DECAY = 0.1
LEARN_RATE = 1e-4
MAX_NORM = 1.0
NORM_EPS = 1e-6
BIAS_ONE = 1.0 - BETA_ONE ** STEP
BIAS_TWO = 1.0 - BETA_TWO ** STEP
TP_COL = P(None, "tp")
ROW_DP = P("dp")
STATE = P("tp", "dp")
ARG_SPECS = (P("dp", None, "tp"), P("dp", "tp"), P("dp", None, "tp"), P("dp", "tp"), ROW_DP, STATE, STATE, STATE)
OUT_SPECS = (TP_COL, P("tp"), TP_COL, P("tp"), P(), STATE, STATE, STATE, P())

MESH = pl.DeviceIdType.MESH
F32 = jnp.float32
BF16 = jnp.bfloat16

Q_TILES = 1920
TILES = 4616
Q_COLS = 15
M_COLS = 8
PART_ROWS = 4614
MAT_ROWS = 36864
WIN = 600
HALF = WIN // 2
WIN_START = (0, 570, 1140, 1725, 2304, 2880, 3456, 4016)
EMIT_START = (0, 585, 1155, 1740, 2312, 2888, 3464, 4040)
EMIT_END = (585, 1155, 1740, 2312, 2888, 3464, 4040, 4616)
Q_BLOCKS = (40, 40, 40, 13, 0, 0, 0, 0)
M_BLOCKS = (0, 0, 0, 50, 75, 75, 75, 75)
EMIT = 588
STATE_BASE = 176
STATE_ROWS = 4984
HALO = 80

K_RS = 5
N_RS = HALF // K_RS
K_AG = 12
N_AG = EMIT // K_AG
STEP_TILES = 4
HALF_AG = K_AG // 2
FLAT = PART_ROWS * 128
CHUNK_ROWS = 64
CHUNK = CHUNK_ROWS * 128
CHUNKS = PART_ROWS // CHUNK_ROWS
TAIL = PART_ROWS - CHUNKS * CHUNK_ROWS
TILE = (8, 128)
VMEM_LIMIT = 50 * 1024 * 1024
STEP_VMEM = 50 * 1024 * 1024
DP, TP = 8, 4
O_START, U_START, D_START, N_START = 1920, 2560, 3584, 4608
S_RAW, S_PF, S_PP, S_SUM, S_HALO, S_N1, S_N2, S_OWN, S_PAIR, S_PASS, SENDS = 0, 8, 9, 11, 13, 16, 17, 18, 21, 24, 25


def fori(count, step, start=0):
    def body(k, carry):
        step(k)
        return carry

    lax.fori_loop(start, count, body, 0)


def lanes(block):
    return pl.ds(pl.multiple_of(block * 128, 128), 128)


PIECE_ORDER = tuple(k // 2 + (K_AG // 2) * (k % 2) for k in range(K_AG))


def piece_blocks():
    table = []
    for k, piece in enumerate(PIECE_ORDER):
        rows = []
        for part in range(8):
            base = EMIT_START[part] - WIN_START[part]
            q_count, m_count = Q_BLOCKS[part], M_BLOCKS[part]

            def after(tile):
                q = min(q_count, max(0, -(-tile // Q_COLS)))
                m = min(m_count, max(0, -(-(tile - q_count * Q_COLS) // M_COLS)))
                return q, m

            def before(tile):
                q = min(q_count, max(0, tile // Q_COLS))
                m = min(m_count, max(0, (tile - q_count * Q_COLS) // M_COLS))
                return q, m

            middle = before(base + (K_AG // 2) * N_AG)
            low = (0, 0) if piece == 0 else middle if piece == K_AG // 2 else after(base + piece * N_AG)
            if piece == K_AG - 1:
                high = (q_count, m_count)
            elif piece == K_AG // 2 - 1:
                high = middle
            else:
                high = after(base + (piece + 1) * N_AG)
            rows.append((low[0], high[0], low[1], high[1]))
        table.append(tuple(zip(*rows)))
    return tuple(table)


PIECE_BLOCKS = piece_blocks()


def pick(values, y, x, c):
    total = 0
    for index, value in enumerate(values):
        if value:
            term = value
            for shift, bit in ((2, y), (1, x), (0, c)):
                term = term * (bit if (index >> shift) & 1 else 1 - bit)
            total = total + term
    return total


def step_kernel(gq, go, gu, gd, gn, w_in, m_in, v_in,
                ag, w_out, m_out, v_out, norm_out,
                grads, q_stage, r_ra, r_rb, r_da, r_db, r_pf, r_pa, r_pb,
                r_sa, r_sb, s_sa, s_sb, gsum, mask, state, flat_w, flat_m, flat_v, halo_w, halo_m, halo_v,
                gn_stage, pbuf, nb1, nb2,
                load_sem, store_sem, own_sem, ss, rs_raw, rs_pf, rs_pp, rs_s, rs_h, rs_n1, rs_n2,
                rs_own, rs_pass, rs_own_pair, rs_pair):
    dp = lax.axis_index("dp")
    tp = lax.axis_index("tp")
    y = dp // 4
    x = dp // 2 % 2
    c = dp % 2

    def at(yy, xx, cc):
        return {"dp": yy * 4 + xx * 2 + cc}

    def win(yy, xx, cc):
        return pick(WIN_START, yy, xx, cc)

    ny, nx, nc = 1 - y, 1 - x, 1 - c

    def remote(src, dst, ssem, rsem, dev):
        return pltpu.make_async_remote_copy(
            src_ref=src, dst_ref=dst, send_sem=ssem, recv_sem=rsem, device_id=dev, device_id_type=MESH)

    flats = (flat_w, flat_m, flat_v)
    halos = (halo_w, halo_m, halo_v)
    load_q = pltpu.make_async_copy(gq, q_stage, load_sem.at[0])
    loads = [pltpu.make_async_copy(gn, gn_stage, load_sem.at[1])]
    for index, (src, start, end) in enumerate(((go, O_START, U_START), (gu, U_START, D_START), (gd, D_START, N_START))):
        loads.append(pltpu.make_async_copy(src, grads.at[pl.ds(start, end - start)], load_sem.at[2 + index]))
    state_loads = [pltpu.make_async_copy(src, flats[index], load_sem.at[5 + index])
                   for index, src in enumerate((w_in, m_in, v_in))]
    barrier = pltpu.get_barrier_semaphore()
    load_q.start()
    for copy in loads:
        copy.start()
    for offset in range(1, DP):
        pl.semaphore_signal(barrier, inc=1, device_id={"dp": (dp + offset) % DP}, device_id_type=MESH)
    for offset in range(1, TP):
        pl.semaphore_signal(barrier, inc=1, device_id={"tp": (tp + offset) % TP}, device_id_type=MESH)

    first = (4 - 4 * x) * y

    def turn(k):
        block = (k + first) % 8

        def body(col):
            turned = q_stage[lanes(col), lanes(block)].T
            for index in range(16):
                grads[block * 240 + index * Q_COLS + col] = turned[index * 8:(index + 1) * 8]

        fori(Q_COLS, body)

    load_q.wait()
    fori(4, turn)
    for copy in loads:
        copy.wait()
    for col in range(M_COLS):
        rows = gn_stage[:, col * 128:(col + 1) * 128].astype(F32)
        grads[N_START + col] = jnp.concatenate([rows, jnp.zeros((2, 128), F32)], axis=0).astype(BF16)
    pl.semaphore_wait(barrier, DP + TP - 2)

    def cut(start, k, n=N_RS):
        return pl.ds(start + k * n, n)

    raw_bufs = (r_ra, r_rb, r_da, r_db)

    def raw(stream, cc, k):
        to_y = stream in (0, 2)
        half = 0 if to_y else HALF
        if stream < 2:
            start = win(ny, nx, cc)
        elif to_y:
            start = win(ny, x, cc)
        else:
            start = win(y, nx, cc)
        dev = at(ny, x, cc) if to_y else at(y, nx, cc)
        return remote(grads.at[cut(start + half, k)], raw_bufs[stream].at[c, cut(0, k)],
                      ss.at[S_RAW + 2 * stream + cc], rs_raw.at[stream, k], dev)

    partner = at(y, x, nc)

    def partner_final(k):
        return remote(grads.at[cut(win(y, x, nc), k)], r_pf.at[cut(0, k)], ss.at[S_PF], rs_pf.at[k], partner)

    def partner_relay(which, k):
        if which == 0:
            start, dst = win(y, nx, nc), r_pa
        else:
            start, dst = win(ny, x, nc) + HALF, r_pb
        return remote(grads.at[cut(start, k)], dst.at[cut(0, k)], ss.at[S_PP + which], rs_pp.at[which, k], partner)

    def relayed(which, k):
        src, dst, dev = (s_sa, r_sa, at(y, nx, c)) if which == 0 else (s_sb, r_sb, at(ny, x, c))
        return remote(src.at[cut(0, k)], dst.at[cut(0, k)], ss.at[S_SUM + which], rs_s.at[which, k], dev)

    def halo_copy(index):
        src = (w_in, m_in, v_in)[index]
        return remote(src.at[:, pl.ds(0, HALO * 128)], halos[index],
                      ss.at[S_HALO + index], rs_h.at[index], {"dp": (dp + DP - 1) % DP})

    def arrived(buf, sem):
        pltpu.make_async_copy(buf, buf, sem).wait()

    def sent(buf, sem):
        pltpu.make_async_copy(buf, buf, sem).wait()

    def raw_arrived(stream, k):
        arrived(raw_bufs[stream].at[:, cut(0, k)], rs_raw.at[stream, k])

    def send_diag(*which):
        def step(k):
            for stream, cc in which:
                raw(stream, cc, k).start()
        fori(K_RS, step)

    def send_over_y(k):
        raw(2, 0, k).start()
        raw(2, 1, k).start()
        partner_relay(1, k).start()

    def send_over_x(k):
        raw(3, 0, k).start()
        raw(3, 1, k).start()
        partner_relay(0, k).start()
        partner_final(k).start()
        partner_final(k + K_RS).start()

    @pl.when(y == 0)
    def _():
        send_diag((0, 0), (1, 0), (0, 1), (1, 1))
        fori(K_RS, send_over_y)
        fori(8, turn, 4)
        fori(K_RS, send_over_x)

    @pl.when(y == 1)
    def _():
        send_diag((0, 0), (1, 0), (0, 1))
        turn(4)
        send_diag((1, 1))
        fori(K_RS, send_over_x)
        fori(8, turn, 5)
        fori(K_RS, send_over_y)

    for index in range(3):
        halo_copy(index).start()
    for copy in state_loads:
        copy.start()

    off = PART_ROWS * dp - 8 * win(y, x, c)
    mat_end = MAT_ROWS - 8 * win(y, x, c)
    last = jnp.minimum(off + PART_ROWS, mat_end + jnp.where(tp == 0, 48, 0))
    q_blocks = pick(Q_BLOCKS, y, x, c)
    m_blocks = pick(M_BLOCKS, y, x, c)
    row = lax.broadcasted_iota(jnp.int32, TILE, 0)
    mask[pl.ds(WIN - 5, 5)] = jnp.zeros((5, *TILE), F32)

    def mask_blocks(columns, tile0):
        def body(block):
            for col in range(columns):
                tile = tile0 + block * columns + col
                lane_row = row * columns + (tile0 * 8 + block * columns * 8 + col)
                inside = jnp.logical_and(lane_row >= off, lane_row < last)
                mask[tile] = jnp.where(inside, 1.0, 0.0)
        return body

    fori(q_blocks, mask_blocks(Q_COLS, 0))
    fori(m_blocks, mask_blocks(M_COLS, q_blocks * Q_COLS))

    for copy in state_loads:
        copy.wait()

    def flat_part(k):
        return pl.ds(pl.multiple_of(k * CHUNK, CHUNK), CHUNK)

    def row_part(k):
        return pl.ds(STATE_BASE + k * CHUNK_ROWS, CHUNK_ROWS)

    tail_flat = pl.ds(CHUNKS * CHUNK, TAIL * 128)
    tail_rows = pl.ds(STATE_BASE + CHUNKS * CHUNK_ROWS, TAIL)

    def to_rows(k):
        for index in range(3):
            state[index, row_part(k)] = flats[index][:, flat_part(k)].reshape(CHUNK_ROWS, 128)

    fori(CHUNKS, to_rows)
    for index in range(3):
        state[index, tail_rows] = flats[index][:, tail_flat].reshape(TAIL, 128)

    def relay(which):
        own_start = win(y, nx, c) if which == 0 else win(ny, x, c) + HALF
        raw_buf, pair_buf, out_buf = (r_ra, r_pa, s_sa) if which == 0 else (r_rb, r_pb, s_sb)

        def body(k):
            raw_arrived(which, k)
            arrived(pair_buf.at[cut(0, k)], rs_pp.at[which, k])

            def tiles(index):
                here = pl.ds(k * N_RS + index * STEP_TILES, STEP_TILES)
                total = grads[pl.ds(own_start + k * N_RS + index * STEP_TILES, STEP_TILES)].astype(F32)
                total = total + pair_buf[here].astype(F32)
                total = total + raw_buf[0, here].astype(F32)
                total = total + raw_buf[1, here].astype(F32)
                out_buf[here] = total

            fori(N_RS // STEP_TILES, tiles)
            relayed(which, k).start()
        return body

    relay_a, relay_b = relay(0), relay(1)

    def relay_step(k):
        relay_a(k)
        relay_b(k)

    fori(K_RS, relay_step)

    for index in range(3):
        arrived(halos[index], rs_h.at[index])
        state[index, pl.ds(STATE_BASE + PART_ROWS, HALO)] = halos[index][...].reshape(HALO, 128)

    def finish(which):
        half = 0 if which == 0 else HALF
        raw_buf, sum_buf = (r_da, r_sa) if which == 0 else (r_db, r_sb)

        def body(k, acc):
            raw_arrived(2 + which, k)
            arrived(r_pf.at[cut(half, k)], rs_pf.at[k + which * K_RS])
            arrived(sum_buf.at[cut(0, k)], rs_s.at[which, k])

            def tiles(index, acc):
                here = pl.ds(k * N_RS + index * STEP_TILES, STEP_TILES)
                part = pl.ds(half + k * N_RS + index * STEP_TILES, STEP_TILES)
                total = grads[pl.ds(win(y, x, c) + half + k * N_RS + index * STEP_TILES, STEP_TILES)].astype(F32)
                total = total + r_pf[part].astype(F32)
                total = total + raw_buf[0, here].astype(F32)
                total = total + raw_buf[1, here].astype(F32)
                total = (total + sum_buf[here]) * 0.125
                gsum[part] = total
                square = jnp.where(mask[part] > 0.5, total * total, 0.0)
                return acc + jnp.sum(square, axis=0)

            return lax.fori_loop(0, N_RS // STEP_TILES, tiles, acc)
        return body

    finish_a, finish_b = finish(0), finish(1)
    acc = lax.fori_loop(0, K_RS, lambda k, acc: finish_b(k, finish_a(k, acc)), jnp.zeros(TILE, F32))

    nb1[dp] = acc

    for offset in range(1, DP):
        remote(nb1.at[dp], nb1.at[dp], ss.at[S_N1], rs_n1, {"dp": (dp + offset) % DP}).start()
    arrived(nb1.at[pl.ds(0, DP - 1)], rs_n1)
    plane = nb1[0]
    for index in range(1, DP):
        plane = plane + nb1[index]
    nb2[tp] = plane
    for offset in range(1, TP):
        remote(nb2.at[tp], nb2.at[tp], ss.at[S_N2], rs_n2, {"tp": (tp + offset) % TP}).start()
    arrived(nb2.at[pl.ds(0, TP - 1)], rs_n2)
    total = nb2[0] + nb2[1] + nb2[2] + nb2[3]
    total = jnp.sum(jnp.sum(total, axis=0, keepdims=True), axis=1, keepdims=True)
    norm = jnp.sqrt(jnp.broadcast_to(total, TILE))
    norm_out[...] = norm
    clip = jnp.minimum(1.0, MAX_NORM / (norm + NORM_EPS))

    def update_blocks(columns, tile0):
        def body(block):
            row0 = tile0 * 8 + block * columns * 8
            decay = jnp.where(row0 < mat_end, DECAY, 0.0)
            for col in range(columns):
                tile = tile0 + block * columns + col
                here = pl.ds(STATE_BASE - off + row0 + col, 8, stride=columns)
                grad = gsum[tile] * clip
                w_old = state[0, here]
                m_new = BETA_ONE * state[1, here] + (1.0 - BETA_ONE) * grad
                v_new = BETA_TWO * state[2, here] + (1.0 - BETA_TWO) * grad * grad
                step_dir = (m_new * (1.0 / BIAS_ONE)) / (jnp.sqrt(v_new * (1.0 / BIAS_TWO)) + ADAM_EPS)
                w_new = w_old - LEARN_RATE * (step_dir + decay * w_old)
                state[0, here] = w_new
                state[1, here] = m_new
                state[2, here] = v_new
                pbuf[tile] = w_new.astype(BF16)
        return body

    update_q = update_blocks(Q_COLS, 0)
    update_m = update_blocks(M_COLS, q_blocks * Q_COLS)

    emit0 = pick([e - s for e, s in zip(EMIT_START, WIN_START)], y, x, c)

    def piece(k):
        return pl.ds(k * N_AG, N_AG)

    part_x, part_y, part_d = y * 4 + nx * 2 + c, ny * 4 + x * 2 + c, ny * 4 + nx * 2 + c
    dev_x, dev_y = at(y, nx, c), at(ny, x, c)

    def own_out(which, k):
        dev = (dev_x, dev_y, partner)[which]
        rsem = rs_own_pair if which == 2 else rs_own.at[which, k]
        return remote(pbuf.at[pl.ds(emit0 + k * N_AG, N_AG)], ag.at[dp, piece(k)], ss.at[S_OWN + which], rsem, dev)

    def pass_out(which, k):
        part, dev = ((part_x, dev_y), (part_y, dev_x))[which]
        return remote(ag.at[part, piece(k)], ag.at[part, piece(k)], ss.at[S_PASS], rs_pass.at[k], dev)

    def pair_out(which, k):
        part = (part_x, part_y, part_d)[which]
        return remote(ag.at[part, piece(k)], ag.at[part, piece(k)], ss.at[S_PAIR + which], rs_pair.at[which], partner)

    own_copy = pltpu.make_async_copy(pbuf.at[pl.ds(emit0, EMIT)], ag.at[dp], own_sem)

    for k, bounds in enumerate(PIECE_BLOCKS):
        q_from, q_to, m_from, m_to = (pick(bound, y, x, c) for bound in bounds)
        fori(q_to, update_q, q_from)
        fori(m_to, update_m, m_from)
        own_out(k % 2, PIECE_ORDER[k]).start()
        own_out(2, PIECE_ORDER[k]).start()

    def send_rest(k):
        own_out(0, HALF_AG + k).start()
        own_out(1, k).start()

    fori(HALF_AG, send_rest)
    own_copy.start()

    def to_flat(k):
        for index in range(3):
            flats[index][:, flat_part(k)] = state[index, row_part(k)].reshape(1, CHUNK)

    fori(CHUNKS, to_flat)
    stores = []
    for index, dst in enumerate((w_out, m_out, v_out)):
        flats[index][:, tail_flat] = state[index, tail_rows].reshape(1, TAIL * 128)
        stores.append(pltpu.make_async_copy(flats[index], dst, store_sem.at[index]))
        stores[-1].start()

    def first_half(k):
        arrived(ag.at[part_x, piece(k)], rs_own.at[0, k])
        pass_out(0, k).start()
        pair_out(0, k).start()
        later = k + HALF_AG
        arrived(ag.at[part_y, piece(later)], rs_own.at[1, later])
        pass_out(1, later).start()
        pair_out(1, later).start()

    def second_half(k):
        later = k + HALF_AG
        arrived(ag.at[part_x, piece(later)], rs_own.at[0, later])
        pair_out(0, later).start()
        arrived(ag.at[part_y, piece(k)], rs_own.at[1, k])
        pair_out(1, k).start()

    def diagonal(k):
        for index in (k, k + HALF_AG):
            arrived(ag.at[part_d, piece(index)], rs_pass.at[index])
            pair_out(2, index).start()

    fori(HALF_AG, first_half)
    fori(HALF_AG, second_half)
    fori(HALF_AG, diagonal)

    for stream in range(4):
        for cc in range(2):
            sent(raw_bufs[stream].at[0], ss.at[S_RAW + 2 * stream + cc])
    sent(r_pf, ss.at[S_PF])
    for which in range(2):
        sent(r_pa, ss.at[S_PP + which])
        sent(s_sa, ss.at[S_SUM + which])
    for which in range(3):
        sent(halos[which], ss.at[S_HALO + which])
        sent(ag.at[0], ss.at[S_OWN + which])
        sent(ag.at[0], ss.at[S_PAIR + which])
    sent(nb1.at[pl.ds(0, DP - 1)], ss.at[S_N1])
    sent(nb2.at[pl.ds(0, TP - 1)], ss.at[S_N2])
    sent(ag.at[0], ss.at[S_PASS])
    arrived(ag.at[y * 4 + x * 2 + nc], rs_own_pair)
    for which, part in enumerate((y * 4 + nx * 2 + nc, ny * 4 + x * 2 + nc, ny * 4 + nx * 2 + nc)):
        arrived(ag.at[part], rs_pair.at[which])
    own_copy.wait()
    for copy in stores:
        copy.wait()


def pieces_of(start, end):
    found = []
    for part in range(DP):
        low, high = max(start, EMIT_START[part]), min(end, EMIT_END[part])
        if low < high:
            found.append((part, low - EMIT_START[part], low - start, high - low))
    return found


def lay_out_kernel(ag, w_in, m_in, v_in, norm, q_out, o_out, u_out, d_out, n_out, w_out, m_out, v_out, norm_out,
                   tiles, n_tiles, q_stage, flat_w, flat_m, flat_v, in_sem, out_sem, q_sem, flat_sem):
    flats = (flat_w, flat_m, flat_v)

    def ranges(dst, start, end, sem, base):
        return [pltpu.make_async_copy(ag.at[part, pl.ds(low, count)], dst.at[pl.ds(offset, count)], sem.at[base + index])
                for index, (part, low, offset, count) in enumerate(pieces_of(start, end))]

    loads = ranges(tiles, 0, O_START, in_sem, 0)
    loads += ranges(n_tiles, N_START, TILES, in_sem, len(loads))
    outs = []
    for dst, start, end in ((o_out, O_START, U_START), (u_out, U_START, D_START), (d_out, D_START, N_START)):
        outs += ranges(dst, start, end, out_sem, len(outs))
    flat_loads = [pltpu.make_async_copy(src, flats[index], flat_sem.at[index])
                  for index, src in enumerate((w_in, m_in, v_in))]
    flat_stores = [pltpu.make_async_copy(flats[index], dst, flat_sem.at[3 + index])
                   for index, dst in enumerate((w_out, m_out, v_out))]

    def q_store(block):
        return pltpu.make_async_copy(q_stage.at[:, lanes(block)], q_out.at[:, lanes(block)], q_sem.at[block])

    def turn(block):
        def body(col):
            part = jnp.concatenate([tiles[block * 240 + index * Q_COLS + col] for index in range(16)], axis=0)
            q_stage[lanes(col), lanes(block)] = part.T

        fori(Q_COLS, body)
        q_store(block).start()

    for copy in loads + flat_loads + outs:
        copy.start()
    norm_out[0, 0] = jnp.max(norm[...])
    loads[0].wait()
    fori(2, turn)
    loads[1].wait()
    fori(4, turn, 2)
    for index in range(3):
        flat_loads[index].wait()
        flat_stores[index].start()
    for copy in loads[2:]:
        copy.wait()
    fori(8, turn, 4)
    for col in range(M_COLS):
        n_out[:, col * 128:(col + 1) * 128] = n_tiles[col].astype(F32)[:6].astype(BF16)
    for copy in outs + flat_stores:
        copy.wait()
    fori(8, lambda block: q_store(block).wait())


def to_tiles(matrix):
    rows, cols = matrix.shape
    return matrix.reshape(rows // 8, 8, cols // 128, 128).transpose(0, 2, 1, 3).reshape(rows * cols // 1024, 8, 128)


def from_tiles(tiles, rows, cols):
    return tiles.reshape(rows // 8, cols // 128, 8, 128).transpose(0, 2, 1, 3).reshape(rows, cols)


on_chip = pltpu.with_memory_space_constraint


def in_hbm(*arrays):
    return [on_chip(array, pltpu.HBM) for array in arrays]


def any_spec(count):
    return [pl.BlockSpec(memory_space=pltpu.HBM)] * count


def solution(mesh):
    dma = pltpu.SemaphoreType.DMA

    q_shape = (1920, 1024)
    params = functools.partial(pltpu.CompilerParams, vmem_limit_bytes=VMEM_LIMIT)

    def local_step(g_qkv, g_out, g_up, g_down, g_norms, master, mom_one, mom_two):
        gq = g_qkv[0].transpose(1, 2, 3, 0).reshape(q_shape)
        go, gu, gd = to_tiles(g_out[0]), to_tiles(g_up[0]), to_tiles(g_down[0])
        gn = g_norms[0]
        part = jax.ShapeDtypeStruct(master.shape, F32)
        flat = pltpu.VMEM((1, FLAT), F32)
        tile_count = (U_START - O_START, D_START - U_START, N_START - D_START)
        win_f32, half_f32 = pltpu.VMEM((WIN, *TILE), F32), pltpu.VMEM((HALF, *TILE), F32)
        half_bf16 = pltpu.VMEM((HALF, *TILE), BF16)
        scratch = [
            pltpu.VMEM((TILES, *TILE), BF16),
            pltpu.VMEM(q_shape, BF16),
            *[pltpu.VMEM((2, HALF, *TILE), BF16)] * 4,
            pltpu.VMEM((WIN, *TILE), BF16),
            half_bf16, half_bf16, half_f32, half_f32, half_f32, half_f32, win_f32, win_f32,
            pltpu.VMEM((3, STATE_ROWS, 128), F32),
            flat, flat, flat,
            *[pltpu.VMEM((1, HALO * 128), F32)] * 3,
            pltpu.VMEM(g_norms.shape[1:], BF16),
            pltpu.VMEM((WIN + 16, *TILE), BF16),
            pltpu.VMEM((DP, *TILE), F32),
            pltpu.VMEM((TP, *TILE), F32),
            dma((8,)), dma((3,)), dma(()), dma((SENDS,)),
            dma((4, K_RS)), dma((2 * K_RS,)), dma((2, K_RS)), dma((2, K_RS)), dma((3,)), dma(()), dma(()),
            dma((2, K_AG)), dma((K_AG,)), dma(()), dma((3,)),
        ]
        ag, w_new, m_new, v_new, norm = pl.pallas_call(
            step_kernel,
            name="reduce_update_gather",
            out_shape=[pltpu.VMEM((DP, EMIT, *TILE), BF16), part, part, part,
                       pltpu.VMEM(TILE, F32)],
            in_specs=any_spec(8),
            out_specs=[pl.BlockSpec(memory_space=pl.ANY)] + any_spec(3) + [pl.BlockSpec(memory_space=pltpu.VMEM)],
            scratch_shapes=scratch,
            compiler_params=params(collective_id=0, has_side_effects=True, vmem_limit_bytes=STEP_VMEM),
        )(*in_hbm(gq, go, gu, gd, gn, master, mom_one, mom_two))
        pq, po, pu, pd, pn, w_new, m_new, v_new, norm = pl.pallas_call(
            lay_out_kernel,
            name="lay_out",
            out_shape=[jax.ShapeDtypeStruct(q_shape, BF16),
                       *[jax.ShapeDtypeStruct((count, *TILE), BF16) for count in tile_count],
                       jax.ShapeDtypeStruct(g_norms.shape[1:], BF16), part, part, part, jax.ShapeDtypeStruct((1, 1), F32)],
            in_specs=[pl.BlockSpec(memory_space=pl.ANY)] + any_spec(3) + [pl.BlockSpec(memory_space=pltpu.VMEM)],
            out_specs=any_spec(4) + [pl.BlockSpec(memory_space=pltpu.VMEM)] + any_spec(3)
            + [pl.BlockSpec(memory_space=pltpu.SMEM)],
            scratch_shapes=[pltpu.VMEM((O_START, *TILE), BF16), pltpu.VMEM((M_COLS, *TILE), BF16),
                            pltpu.VMEM(q_shape, BF16), flat, flat, flat, dma((8,)), dma((12,)), dma((8,)), dma((6,))],
            compiler_params=params(),
        )(on_chip(ag, pltpu.VMEM), *in_hbm(w_new, m_new, v_new), on_chip(norm, pltpu.VMEM))
        p_qkv = pq.reshape(8, 3, 80, 1024).transpose(3, 0, 1, 2)
        return (p_qkv, *[from_tiles(tiles, tiles.shape[0], 1024) for tiles in (po, pu, pd)],
                pn, w_new, m_new, v_new, norm[0, 0])

    return jax.shard_map(local_step, mesh=mesh, in_specs=ARG_SPECS, out_specs=OUT_SPECS, check_vma=False)
```

time: 1010 us -> 156 us (0.15); the launches traced: 997 us -> 156 us
  other arithmetic: 584 us -> 0 us
  local copies, waits for them, and re-layouts: 195 us -> 0 us
  waiting for transfers between devices: 156 us -> 0 us
  Pallas kernels: 0 us -> 155 us
  blocking collectives: 40.4 us -> 0 us
  between operations: 16.2 us -> 0.65 us
    all_to_all x1 -> x0, other arithmetic: 202 us -> none  [local_step(): lax.all_to_all(flat_grad.reshape(dp_size, part_len), 'dp', 0, 0, tiled=True)]
    all_gather x1 -> x0, other arithmetic: 202 us -> none  [local_step(): lax.all_gather(master_new.astype(jnp.bfloat16), 'dp', axis=0, tiled=True)]
    pallas_call x0 -> x2, Pallas kernels: none -> 155 us  [the longest x1 143 us: local_step(): pl.pallas_call(step_kernel, name='reduce_update_gather', out_shape=[pltpu...]
    unnamed x27 -> x0, local copies, waits for them, and re-layouts: 125 us -> none
    reduce_sum x2 -> x0, other arithmetic: 100 us -> none  [the longest x1 99.1 us: local_step(): grad_mean = jnp.sum(received, axis=0, dtype=jnp.float32) / dp_size]
    all_gather x1 -> x0, waiting for transfers between devices: 78.1 us -> none  [local_step(): lax.all_gather(master_new.astype(jnp.bfloat16), 'dp', axis=0, tiled=True)]
    all_to_all x1 -> x0, waiting for transfers between devices: 77.8 us -> none  [local_step(): lax.all_to_all(flat_grad.reshape(dp_size, part_len), 'dp', 0, 0, tiled=True)]
    psum x1 -> x0, blocking collectives: 40.4 us -> none  [local_step(): grad_norm = jnp.sqrt(lax.psum(local_sq, ('tp', 'dp')))]
  transfers between devices with their start and end apart: 2 -> 0, of which waited for: 2 -> 0; matrix products, arithmetic and copies ran while one was open for 5% -> 0% of each run, Pallas kernels for 0% -> 0%
where the time goes in v2:
time: 156 us
  Pallas kernels  155 us (99%)
    pallas_call x1, Pallas kernels, local_step(): pl.pallas_call(step_kernel, name='reduce_update_gather', out_shape=[pltpu...  143 us
    pallas_call x1, Pallas kernels, local_step(): pl.pallas_call(lay_out_kernel, name='lay_out', out_shape=[jax.ShapeDtypeS...  12.8 us

profile of v2, /device:TPU:0, one launch (start us, length us, event | category | flops | bytes accessed | tf_op | source)
XLA Modules:
  0.0 156.0 jit_solution(13898190398087263874)
XLA Ops:
  0.6 142.6 %reduce_update_gather.1 = (bf16[8,588,8,128]{3,2,1,0:T(8,128)(2,1)S(1)}, f32[1,590592]{1,0:T(1,128)}, f32[1,590592]{1,0:T(1,128)}, f32[1,590592]{1,0:T(1,128)}, f32[8,128]{1,0:T(8,128)S(1)}) custom-call(bf16[1920,1024]{1,0:T(8,128)(2,1)} %bitcast.40, bf16[640,8,128]{2,1,0:T(8,128)(2,1)} %bitcast.43, bf16[1024,8,128]{2,1,0:T(8,128)(2,1)} %bitcast.41, ...), custom_call_target="tpu_custom_call" | custom-call | tf_op jit(solution)/shard_map/reduce_update_gather/pallas_call | solution.py:621
  143.2 12.8 %lay_out.1 = (bf16[1920,1024]{1,0:T(8,128)(2,1)}, bf16[640,8,128]{2,1,0:T(8,128)(2,1)}, bf16[1024,8,128]{2,1,0:T(8,128)(2,1)}, bf16[1024,8,128]{2,1,0:T(8,128)(2...) custom-call(bf16[8,588,8,128]{3,2,1,0:T(8,128)(2,1)S(1)} %get-tuple-, ...), custom_call_target="tpu_custom_call" | custom-call | tf_op jit(solution)/shard_map/lay_out/pallas_call | solution.py:631

commit v3 on v2

--- a/solution.py
+++ b/solution.py
@@ -57,8 +57,9 @@
 CHUNKS = PART_ROWS // CHUNK_ROWS
 TAIL = PART_ROWS - CHUNKS * CHUNK_ROWS
 TILE = (8, 128)
-VMEM_LIMIT = 50 * 1024 * 1024
-STEP_VMEM = 50 * 1024 * 1024
+TURN_UNROLL = 5
+VMEM_LIMIT = 43 * 1024 * 1024
+STEP_VMEM = 43 * 1024 * 1024
 DP, TP = 8, 4
 O_START, U_START, D_START, N_START = 1920, 2560, 3584, 4608
 S_RAW, S_PF, S_PP, S_SUM, S_HALO, S_N1, S_N2, S_OWN, S_PAIR, S_PASS, SENDS = 0, 8, 9, 11, 13, 16, 17, 18, 21, 24, 25
@@ -127,7 +128,7 @@
 def step_kernel(gq, go, gu, gd, gn, w_in, m_in, v_in,
                 ag, w_out, m_out, v_out, norm_out,
                 grads, q_stage, r_ra, r_rb, r_da, r_db, r_pf, r_pa, r_pb,
-                r_sa, r_sb, s_sa, s_sb, gsum, mask, state, flat_w, flat_m, flat_v, halo_w, halo_m, halo_v,
+                r_sa, r_sb, s_sa, s_sb, gsum, mask, state, flat_buf, halo_w, halo_m, halo_v,
                 gn_stage, pbuf, nb1, nb2,
                 load_sem, store_sem, own_sem, ss, rs_raw, rs_pf, rs_pp, rs_s, rs_h, rs_n1, rs_n2,
                 rs_own, rs_pass, rs_own_pair, rs_pair):
@@ -149,13 +150,12 @@
         return pltpu.make_async_remote_copy(
             src_ref=src, dst_ref=dst, send_sem=ssem, recv_sem=rsem, device_id=dev, device_id_type=MESH)
 
-    flats = (flat_w, flat_m, flat_v)
     halos = (halo_w, halo_m, halo_v)
     load_q = pltpu.make_async_copy(gq, q_stage, load_sem.at[0])
     loads = [pltpu.make_async_copy(gn, gn_stage, load_sem.at[1])]
     for index, (src, start, end) in enumerate(((go, O_START, U_START), (gu, U_START, D_START), (gd, D_START, N_START))):
         loads.append(pltpu.make_async_copy(src, grads.at[pl.ds(start, end - start)], load_sem.at[2 + index]))
-    state_loads = [pltpu.make_async_copy(src, flats[index], load_sem.at[5 + index])
+    state_loads = [pltpu.make_async_copy(src, flat_buf, load_sem.at[5 + index])
                    for index, src in enumerate((w_in, m_in, v_in))]
     barrier = pltpu.get_barrier_semaphore()
     load_q.start()
@@ -271,8 +271,7 @@
 
     for index in range(3):
         halo_copy(index).start()
-    for copy in state_loads:
-        copy.start()
+    state_loads[0].start()
 
     off = PART_ROWS * dp - 8 * win(y, x, c)
     mat_end = MAT_ROWS - 8 * win(y, x, c)
@@ -294,9 +293,6 @@
     fori(q_blocks, mask_blocks(Q_COLS, 0))
     fori(m_blocks, mask_blocks(M_COLS, q_blocks * Q_COLS))
 
-    for copy in state_loads:
-        copy.wait()
-
     def flat_part(k):
         return pl.ds(pl.multiple_of(k * CHUNK, CHUNK), CHUNK)
 
@@ -306,13 +302,15 @@
     tail_flat = pl.ds(CHUNKS * CHUNK, TAIL * 128)
     tail_rows = pl.ds(STATE_BASE + CHUNKS * CHUNK_ROWS, TAIL)
 
-    def to_rows(k):
-        for index in range(3):
-            state[index, row_part(k)] = flats[index][:, flat_part(k)].reshape(CHUNK_ROWS, 128)
-
-    fori(CHUNKS, to_rows)
     for index in range(3):
-        state[index, tail_rows] = flats[index][:, tail_flat].reshape(TAIL, 128)
+        def to_rows(k):
+            state[index, row_part(k)] = flat_buf[:, flat_part(k)].reshape(CHUNK_ROWS, 128)
+
+        state_loads[index].wait()
+        fori(CHUNKS, to_rows)
+        state[index, tail_rows] = flat_buf[:, tail_flat].reshape(TAIL, 128)
+        if index < 2:
+            state_loads[index + 1].start()
 
     def relay(which):
         own_start = win(y, nx, c) if which == 0 else win(ny, x, c) + HALF
@@ -450,16 +448,15 @@
     fori(HALF_AG, send_rest)
     own_copy.start()
 
-    def to_flat(k):
-        for index in range(3):
-            flats[index][:, flat_part(k)] = state[index, row_part(k)].reshape(1, CHUNK)
-
-    fori(CHUNKS, to_flat)
-    stores = []
-    for index, dst in enumerate((w_out, m_out, v_out)):
-        flats[index][:, tail_flat] = state[index, tail_rows].reshape(1, TAIL * 128)
-        stores.append(pltpu.make_async_copy(flats[index], dst, store_sem.at[index]))
-        stores[-1].start()
+    def store_state(index):
+        def to_flat(k):
+            flat_buf[:, flat_part(k)] = state[index, row_part(k)].reshape(1, CHUNK)
+
+        fori(CHUNKS, to_flat)
+        flat_buf[:, tail_flat] = state[index, tail_rows].reshape(1, TAIL * 128)
+        copy = pltpu.make_async_copy(flat_buf, (w_out, m_out, v_out)[index], store_sem.at[index])
+        copy.start()
+        return copy
 
     def first_half(k):
         arrived(ag.at[part_x, piece(k)], rs_own.at[0, k])
@@ -482,9 +479,10 @@
             arrived(ag.at[part_d, piece(index)], rs_pass.at[index])
             pair_out(2, index).start()
 
-    fori(HALF_AG, first_half)
-    fori(HALF_AG, second_half)
-    fori(HALF_AG, diagonal)
+    for index, step in enumerate((first_half, second_half, diagonal)):
+        store = store_state(index)
+        fori(HALF_AG, step)
+        store.wait()
 
     for stream in range(4):
         for cc in range(2):
@@ -504,8 +502,6 @@
     for which, part in enumerate((y * 4 + nx * 2 + nc, ny * 4 + x * 2 + nc, ny * 4 + nx * 2 + nc)):
         arrived(ag.at[part], rs_pair.at[which])
     own_copy.wait()
-    for copy in stores:
-        copy.wait()
 
 
 def pieces_of(start, end):
@@ -518,50 +514,46 @@
 
 
 def lay_out_kernel(ag, w_in, m_in, v_in, norm, q_out, o_out, u_out, d_out, n_out, w_out, m_out, v_out, norm_out,
-                   tiles, n_tiles, q_stage, flat_w, flat_m, flat_v, in_sem, out_sem, q_sem, flat_sem):
-    flats = (flat_w, flat_m, flat_v)
-
-    def ranges(dst, start, end, sem, base):
-        return [pltpu.make_async_copy(ag.at[part, pl.ds(low, count)], dst.at[pl.ds(offset, count)], sem.at[base + index])
+                   q_stage, out_sem, q_sem, flat_sem):
+    def ranges(dst, start, end, base):
+        return [pltpu.make_async_copy(ag.at[pl.ds(part * EMIT + low, count)], dst.at[pl.ds(offset, count)], out_sem.at[base + index])
                 for index, (part, low, offset, count) in enumerate(pieces_of(start, end))]
 
-    loads = ranges(tiles, 0, O_START, in_sem, 0)
-    loads += ranges(n_tiles, N_START, TILES, in_sem, len(loads))
     outs = []
     for dst, start, end in ((o_out, O_START, U_START), (u_out, U_START, D_START), (d_out, D_START, N_START)):
-        outs += ranges(dst, start, end, out_sem, len(outs))
-    flat_loads = [pltpu.make_async_copy(src, flats[index], flat_sem.at[index])
-                  for index, src in enumerate((w_in, m_in, v_in))]
-    flat_stores = [pltpu.make_async_copy(flats[index], dst, flat_sem.at[3 + index])
-                   for index, dst in enumerate((w_out, m_out, v_out))]
+        outs += ranges(dst, start, end, len(outs))
+    for index, (src, dst) in enumerate(((w_in, w_out), (m_in, m_out), (v_in, v_out))):
+        outs.append(pltpu.make_async_copy(src, dst, flat_sem.at[index]))
 
     def q_store(block):
         return pltpu.make_async_copy(q_stage.at[:, lanes(block)], q_out.at[:, lanes(block)], q_sem.at[block])
 
+    def row_start(row):
+        start = row * Q_COLS
+        for part in range(1, 4):
+            gap = EMIT - (EMIT_END[part - 1] - EMIT_START[part - 1])
+            start = start + jnp.where(row * Q_COLS >= EMIT_START[part], gap, 0)
+        return start
+
     def turn(block):
-        def body(col):
-            part = jnp.concatenate([tiles[block * 240 + index * Q_COLS + col] for index in range(16)], axis=0)
-            q_stage[lanes(col), lanes(block)] = part.T
-
-        fori(Q_COLS, body)
+        starts = [row_start(block * 16 + index) for index in range(16)]
+
+        def body(group):
+            for index in range(TURN_UNROLL):
+                col = group * TURN_UNROLL + index
+                part = jnp.concatenate([ag[start + col].astype(F32) for start in starts], axis=0)
+                q_stage[lanes(col), lanes(block)] = part.T.astype(BF16)
+
+        fori(Q_COLS // TURN_UNROLL, body)
         q_store(block).start()
 
-    for copy in loads + flat_loads + outs:
+    for copy in outs:
         copy.start()
     norm_out[0, 0] = jnp.max(norm[...])
-    loads[0].wait()
-    fori(2, turn)
-    loads[1].wait()
-    fori(4, turn, 2)
-    for index in range(3):
-        flat_loads[index].wait()
-        flat_stores[index].start()
-    for copy in loads[2:]:
-        copy.wait()
-    fori(8, turn, 4)
+    fori(8, turn)
     for col in range(M_COLS):
-        n_out[:, col * 128:(col + 1) * 128] = n_tiles[col].astype(F32)[:6].astype(BF16)
-    for copy in outs + flat_stores:
+        n_out[:, col * 128:(col + 1) * 128] = ag[(DP - 1) * EMIT + N_START - EMIT_START[-1] + col].astype(F32)[:6].astype(BF16)
+    for copy in outs:
         copy.wait()
     fori(8, lambda block: q_store(block).wait())
 
@@ -608,7 +600,7 @@
             pltpu.VMEM((WIN, *TILE), BF16),
             half_bf16, half_bf16, half_f32, half_f32, half_f32, half_f32, win_f32, win_f32,
             pltpu.VMEM((3, STATE_ROWS, 128), F32),
-            flat, flat, flat,
+            flat,
             *[pltpu.VMEM((1, HALO * 128), F32)] * 3,
             pltpu.VMEM(g_norms.shape[1:], BF16),
             pltpu.VMEM((WIN + 16, *TILE), BF16),
@@ -621,10 +613,10 @@
         ag, w_new, m_new, v_new, norm = pl.pallas_call(
             step_kernel,
             name="reduce_update_gather",
-            out_shape=[pltpu.VMEM((DP, EMIT, *TILE), BF16), part, part, part,
+            out_shape=[pltpu.VMEM((DP, EMIT, *TILE), BF16), flat, flat, flat,
                        pltpu.VMEM(TILE, F32)],
             in_specs=any_spec(8),
-            out_specs=[pl.BlockSpec(memory_space=pl.ANY)] + any_spec(3) + [pl.BlockSpec(memory_space=pltpu.VMEM)],
+            out_specs=[pl.BlockSpec(memory_space=pl.ANY)] * 4 + [pl.BlockSpec(memory_space=pltpu.VMEM)],
             scratch_shapes=scratch,
             compiler_params=params(collective_id=0, has_side_effects=True, vmem_limit_bytes=STEP_VMEM),
         )(*in_hbm(gq, go, gu, gd, gn, master, mom_one, mom_two))
@@ -634,13 +626,12 @@
             out_shape=[jax.ShapeDtypeStruct(q_shape, BF16),
                        *[jax.ShapeDtypeStruct((count, *TILE), BF16) for count in tile_count],
                        jax.ShapeDtypeStruct(g_norms.shape[1:], BF16), part, part, part, jax.ShapeDtypeStruct((1, 1), F32)],
-            in_specs=[pl.BlockSpec(memory_space=pl.ANY)] + any_spec(3) + [pl.BlockSpec(memory_space=pltpu.VMEM)],
+            in_specs=[pl.BlockSpec(memory_space=pltpu.VMEM)] * 5,
             out_specs=any_spec(4) + [pl.BlockSpec(memory_space=pltpu.VMEM)] + any_spec(3)
             + [pl.BlockSpec(memory_space=pltpu.SMEM)],
-            scratch_shapes=[pltpu.VMEM((O_START, *TILE), BF16), pltpu.VMEM((M_COLS, *TILE), BF16),
-                            pltpu.VMEM(q_shape, BF16), flat, flat, flat, dma((8,)), dma((12,)), dma((8,)), dma((6,))],
+            scratch_shapes=[pltpu.VMEM(q_shape, BF16), dma((12,)), dma((8,)), dma((3,))],
             compiler_params=params(),
-        )(on_chip(ag, pltpu.VMEM), *in_hbm(w_new, m_new, v_new), on_chip(norm, pltpu.VMEM))
+        )(*[on_chip(array, pltpu.VMEM) for array in (ag.reshape(DP * EMIT, *TILE), w_new, m_new, v_new, norm)])
         p_qkv = pq.reshape(8, 3, 80, 1024).transpose(3, 0, 1, 2)
         return (p_qkv, *[from_tiles(tiles, tiles.shape[0], 1024) for tiles in (po, pu, pd)],
                 pn, w_new, m_new, v_new, norm[0, 0])

time: 156 us -> 150 us (0.962)
  Pallas kernels: 155 us -> 149 us
    pallas_call x1, Pallas kernels: 12.8 us -> 6.58 us  [local_step(): pl.pallas_call(lay_out_kernel, name='lay_out', out_shape=[jax.ShapeDtypeS...]
where the time goes in v3:
time: 150 us
  Pallas kernels  149 us (99%)
    pallas_call x1, Pallas kernels, local_step(): pl.pallas_call(step_kernel, name='reduce_update_gather', out_shape=[pltpu...  143 us
    pallas_call x1, Pallas kernels, local_step(): pl.pallas_call(lay_out_kernel, name='lay_out', out_shape=[jax.ShapeDtypeS...  6.58 us

profile of v3, /device:TPU:0, one launch (start us, length us, event | category | flops | bytes accessed | tf_op | source)
XLA Modules:
  0.0 149.8 jit_solution(2192878711180810077)
XLA Ops:
  0.6 142.6 %reduce_update_gather.1 = (bf16[8,588,8,128]{3,2,1,0:T(8,128)(2,1)S(1)}, f32[1,590592]{1,0:T(1,128)S(1)}, f32[1,590592]{1,0:T(1,128)S(1)}, f32[1,590592]{1,0:T(1,128)S(1)}, f32[8,128]{1,0:T(8,128)S(1)}) custom-call(bf16[1920,1024]{1,0:T(8,128)(2,1)} %bitcast.42, bf16[640,8,128]{2,1,0:T(8,128)(2,1)} %bitcast.45, bf16[1024,8,128]{2,1,0:T(8,128)(2,1)} %bitcast.43, ...), custom_call_target="tpu_custom_call" | custom-call | tf_op jit(solution)/shard_map/reduce_update_gather/pallas_call | solution.py:613
  143.2 6.6 %lay_out.1 = (bf16[1920,1024]{1,0:T(8,128)(2,1)}, bf16[640,8,128]{2,1,0:T(8,128)(2,1)}, bf16[1024,8,128]{2,1,0:T(8,128)(2,1)}, bf16[1024,8,128]{2,1,0:T(8,128)(2...) custom-call(bf16[4704,8,128]{2,1,0:T(8,128)(2,1)S(1)} %bitcast.41, ...), custom_call_target="tpu_custom_call" | custom-call | tf_op jit(solution)/shard_map/lay_out/pallas_call | solution.py:623

commit v4 on v3

--- a/solution.py
+++ b/solution.py
@@ -179,7 +179,7 @@
         fori(Q_COLS, body)
 
     load_q.wait()
-    fori(4, turn)
+    fori(2, turn)
     for copy in loads:
         copy.wait()
     for col in range(M_COLS):
@@ -257,15 +257,15 @@
     def _():
         send_diag((0, 0), (1, 0), (0, 1), (1, 1))
         fori(K_RS, send_over_y)
-        fori(8, turn, 4)
+        fori(8, turn, 2)
         fori(K_RS, send_over_x)
 
     @pl.when(y == 1)
     def _():
-        send_diag((0, 0), (1, 0), (0, 1))
-        turn(4)
-        send_diag((1, 1))
+        send_diag((0, 0))
         fori(K_RS, send_over_x)
+        fori(5, turn, 2)
+        send_diag((0, 1), (1, 0), (1, 1))
         fori(8, turn, 5)
         fori(K_RS, send_over_y)
 

time: 150 us -> 148 us (0.987)
  Pallas kernels: 149 us -> 147 us
    pallas_call x1, Pallas kernels: 143 us -> 140 us  [local_step(): pl.pallas_call(step_kernel, name='reduce_update_gather', out_shape=[pltpu...]
where the time goes in v4:
time: 148 us
  Pallas kernels  147 us (99%)
    pallas_call x1, Pallas kernels, local_step(): pl.pallas_call(step_kernel, name='reduce_update_gather', out_shape=[pltpu...  140 us
    pallas_call x1, Pallas kernels, local_step(): pl.pallas_call(lay_out_kernel, name='lay_out', out_shape=[jax.ShapeDtypeS...  6.58 us

profile of v4, /device:TPU:0, one launch (start us, length us, event | category | flops | bytes accessed | tf_op | source)
XLA Modules:
  0.0 147.6 jit_solution(11812790657385150014)
XLA Ops:
  0.6 140.4 %reduce_update_gather.1 = (bf16[8,588,8,128]{3,2,1,0:T(8,128)(2,1)S(1)}, f32[1,590592]{1,0:T(1,128)S(1)}, f32[1,590592]{1,0:T(1,128)S(1)}, f32[1,590592]{1,0:T(1,128)S(1)}, f32[8,128]{1,0:T(8,128)S(1)}) custom-call(bf16[1920,1024]{1,0:T(8,128)(2,1)} %bitcast.42, bf16[640,8,128]{2,1,0:T(8,128)(2,1)} %bitcast.45, bf16[1024,8,128]{2,1,0:T(8,128)(2,1)} %bitcast.43, ...), custom_call_target="tpu_custom_call" | custom-call | tf_op jit(solution)/shard_map/reduce_update_gather/pallas_call | solution.py:613
  141.0 6.6 %lay_out.1 = (bf16[1920,1024]{1,0:T(8,128)(2,1)}, bf16[640,8,128]{2,1,0:T(8,128)(2,1)}, bf16[1024,8,128]{2,1,0:T(8,128)(2,1)}, bf16[1024,8,128]{2,1,0:T(8,128)(2...) custom-call(bf16[4704,8,128]{2,1,0:T(8,128)(2,1)S(1)} %bitcast.41, ...), custom_call_target="tpu_custom_call" | custom-call | tf_op jit(solution)/shard_map/lay_out/pallas_call | solution.py:623
